TPU v7x, 32 devices: a 4x4x1 block of a 4x4x8 slice. The times are simulated.
32 devices in a mesh: rep: 1 (over z), tp: 4 (over y), sp: 8 (over x, core).
Axes of the slice: x: 4, y: 4, z: 1, core: 2. Of those that a mesh axis runs over, the one named last changes fastest.
The devices are a block of a 4x4x8 slice.
Arguments:
- x_in: bfloat16 [8192, 4096], P(('rep', 'sp'))
- positions: int32 [8192], P(('rep', 'sp'))
- norm_gain: float32 [4096], replicated
- w_q: bfloat16 [4096, 4096], P(None, 'tp')
- w_k: bfloat16 [4096, 1024], P(None, 'tp')
- w_v: bfloat16 [4096, 1024], P(None, 'tp')
- w_o: bfloat16 [4096, 4096], P('tp')
- w_gate: bfloat16 [4096, 14336], P(None, 'tp')
- w_up: bfloat16 [4096, 14336], P(None, 'tp')
- w_down: bfloat16 [14336, 4096], P('tp')
Outputs:
- output 1: bfloat16 [8192, 4096], P(('rep', 'sp'))
- output 2: bfloat16 [8192, 32, 128], P('rep', ('tp', 'sp'))
- output 3: bfloat16 [8192, 32, 128], P('rep', ('tp', 'sp'))
All inputs are finite; a program needn't handle non-finite values.
Results may differ from a plain program's by a relative error of at most 0.00226143.
Values are sent between devices in bfloat16 or wider.
A program may use at most 768 MiB of HBM per device.

v0:
```python
import jax
import jax.numpy as jnp
from jax import lax
from jax.sharding import PartitionSpec as P

HEAD_DIM = 128
EPS = 1e-6
ROPE_BASE = 500000.0
SCORE_SCALE = HEAD_DIM ** -0.5


def rms_norm(x_in, norm_gain):
    x_f32 = x_in.astype(jnp.float32)
    inv_rms = lax.rsqrt(jnp.mean(x_f32 * x_f32, axis=-1, keepdims=True) + EPS)
    return (x_f32 * inv_rms * norm_gain).astype(jnp.bfloat16)


def rope_tables(positions):
    inv_freq = ROPE_BASE ** (-(jnp.arange(HEAD_DIM // 2, dtype=jnp.float32) * (2.0 / HEAD_DIM)))
    angles = positions.astype(jnp.float32)[:, None] * inv_freq[None, :]
    return jnp.cos(angles)[:, None, :], jnp.sin(angles)[:, None, :]


def rotate(vectors, cos_tab, sin_tab):
    half_dim = HEAD_DIM // 2
    lower_part = vectors[..., :half_dim]
    upper_part = vectors[..., half_dim:]
    return jnp.concatenate([lower_part * cos_tab - upper_part * sin_tab, upper_part * cos_tab + lower_part * sin_tab], axis=-1).astype(jnp.bfloat16)


def gated_mlp(normed, w_gate, w_up, w_down):
    gate_acc = jnp.dot(normed, w_gate, preferred_element_type=jnp.float32)
    up_acc = jnp.dot(normed, w_up, preferred_element_type=jnp.float32)
    hidden = (jax.nn.silu(gate_acc) * up_acc).astype(jnp.bfloat16)
    return jnp.dot(hidden, w_down, preferred_element_type=jnp.float32)


def causal_attention(q_rows, k_keys, v_keys, q_offset):
    tokens_q = q_rows.shape[0]
    heads_here = q_rows.shape[1]
    key_count = k_keys.shape[0]
    cache_here = k_keys.shape[1]
    group_size = heads_here // cache_here
    tile_rows = min(tokens_q, 128)
    key_idx = jnp.arange(key_count)

    def attend_tile(tile_id):
        q_tile = lax.dynamic_slice_in_dim(q_rows, tile_id * tile_rows, tile_rows, axis=0).reshape(tile_rows, cache_here, group_size, HEAD_DIM)
        scores = jnp.einsum("qcgd,kcd->cgqk", q_tile, k_keys, preferred_element_type=jnp.float32) * SCORE_SCALE
        query_idx = q_offset + tile_id * tile_rows + jnp.arange(tile_rows)
        scores = jnp.where(key_idx[None, :] <= query_idx[:, None], scores, -jnp.inf)
        weights = jnp.exp(scores - jnp.max(scores, axis=-1, keepdims=True))
        weight_total = jnp.sum(weights, axis=-1)
        weighted_sum = jnp.einsum("cgqk,kcd->qcgd", weights.astype(jnp.bfloat16), v_keys, preferred_element_type=jnp.float32)
        return (weighted_sum / jnp.transpose(weight_total, (2, 0, 1))[..., None]).astype(jnp.bfloat16)

    attn_tiles = lax.map(attend_tile, jnp.arange(tokens_q // tile_rows))
    return attn_tiles.reshape(tokens_q, heads_here, HEAD_DIM)


def solution(mesh):
    sp_size = mesh.shape["sp"]
    row_spec = P(("rep", "sp"), None)
    cache_spec = P("rep", ("tp", "sp"), None)

    def layer_block(x_in, positions, norm_gain, w_q, w_k, w_v, w_o, w_gate, w_up, w_down):
        tok_local = x_in.shape[0]
        heads_tp = w_q.shape[1] // HEAD_DIM
        kv_tp = w_k.shape[1] // HEAD_DIM
        heads_dev = heads_tp // sp_size
        cache_tp = max(kv_tp, sp_size)
        cache_dev = cache_tp // sp_size
        kv_repeat = cache_tp // kv_tp
        normed = rms_norm(x_in, norm_gain)
        cos_tab, sin_tab = rope_tables(positions)
        q_rot = rotate(jnp.dot(normed, w_q, preferred_element_type=jnp.float32).reshape(tok_local, heads_tp, HEAD_DIM), cos_tab, sin_tab)
        k_rot = rotate(jnp.dot(normed, w_k, preferred_element_type=jnp.float32).reshape(tok_local, kv_tp, HEAD_DIM), cos_tab, sin_tab)
        v_val = jnp.dot(normed, w_v, preferred_element_type=jnp.float32).astype(jnp.bfloat16).reshape(tok_local, kv_tp, HEAD_DIM)
        q_send = q_rot.reshape(tok_local, sp_size, heads_dev, HEAD_DIM)
        k_send = jnp.repeat(k_rot, kv_repeat, axis=1).reshape(tok_local, sp_size, cache_dev, HEAD_DIM)
        v_send = jnp.repeat(v_val, kv_repeat, axis=1).reshape(tok_local, sp_size, cache_dev, HEAD_DIM)
        send_buf = jnp.concatenate([q_send, k_send, v_send], axis=2)
        recv_buf = lax.all_to_all(send_buf, "sp", 1, 0, tiled=True)
        recv_buf = recv_buf.reshape(tok_local * sp_size, heads_dev + 2 * cache_dev, HEAD_DIM)
        q_all = recv_buf[:, :heads_dev]
        k_all = recv_buf[:, heads_dev:heads_dev + cache_dev]
        v_all = recv_buf[:, heads_dev + cache_dev:]
        attn_heads = causal_attention(q_all, k_all, v_all, 0)
        attn_tok = lax.all_to_all(attn_heads, "sp", 0, 1, tiled=True).reshape(tok_local, heads_tp * HEAD_DIM)
        attn_sum = lax.psum(jnp.dot(attn_tok, w_o, preferred_element_type=jnp.float32), "tp")
        mlp_sum = lax.psum(gated_mlp(normed, w_gate, w_up, w_down), "tp")
        y_out = (x_in.astype(jnp.float32) + attn_sum + mlp_sum).astype(jnp.bfloat16)
        return y_out, k_all, v_all

    return jax.shard_map(
        layer_block,
        mesh=mesh,
        in_specs=(row_spec, P(("rep", "sp")), P(None), P(None, "tp"), P(None, "tp"), P(None, "tp"), P("tp", None), P(None, "tp"), P(None, "tp"), P("tp", None)),
        out_specs=(row_spec, cache_spec, cache_spec),
        check_vma=False,
    )
```

profile of v0, /device:TPU:97, one launch (start us, length us, event | category | flops | bytes accessed | tf_op | source)
XLA Modules:
  0.0 1202.5 jit_solution(10909497586804063909)
XLA Ops:
  8.1 5.5 fusion.40
  13.6 2.9 convolution_convert_fusion
  16.5 2.9 fusion.55
  19.5 14.2 %fusion.57 = f32[1024,1024]{0,1:T(8,128)S(1)} fusion(bf16[4096,1024]{1,0:T(8,128)(2,1)} %param.15, bf16[1024,4096]{1,0:T(8,128)(2,1)} %param.12, f32[4096]{0:T(1024)S(1)} %copy-done.5, f32[1024]{0:T(1024)S(1)} %add_rsqrt_fusion), kind=kOutput, calls=%fused_computation.49 | convolution fusion | flops 8606711808 | bytes 20992000 | tf_op jit(solution)/shard_map/dot_general | solution.py:76
  36.1 3.1 pad_maximum_fusion
  39.3 7.0 all-to-all-start
  46.3 35.6 %fusion.52 = f32[1024,3584]{1,0:T(8,128)S(1)} fusion(bf16[4096,3584]{1,0:T(8,128)(2,1)} %param.19, bf16[1024,4096]{1,0:T(8,128)(2,1)} %param.12, f32[4096]{0:T(1024)S(1)} %copy-done.5, f32[1024]{0:T(1024)S(1)} %add_rsqrt_fusion), kind=kOutput, calls=%fused_computation.47 | convolution fusion | flops 30081548288 | bytes 52449280 | tf_op jit(solution)/shard_map/dot_general | solution.py:32
  82.0 39.3 %multiply_convert_fusion.clone.4 = bf16[1024,3584]{1,0:T(8,128)(2,1)} fusion(f32[1024,3584]{1,0:T(8,128)S(1)} %fusion.52, bf16[4096,3584]{1,0:T(8,128)(2,1)} %param.20, bf16[1024,4096]{1,0:T(8,128)(2,1)} %param.12, f32[4096]{0:T(1024)S(1)} %copy-done.5, f32[1024]{0:T(1024)S(1)} %add_rsqrt_fusion), kind=kOutput, calls=%fused_computation.30.clone.clone.clone.1 | convolution fusion | flops 30103568384 | bytes 59789312 | tf_op jit(solution)/shard_map/dot_general | solution.py:33
  121.3 8.6 copy.23
  129.9 5.3 fusion.60
  135.1 398.2 %while.11 = (s32[]{:T(128)}, bf16[64,128,1,1,128]{4,1,3,2,0:T(8,128)(2,1)}, s32[64]{0:T(128)S(1)}, bf16[8192,1,128]{2,0,1:T(8,128)(2,1)}, bf16[8192,1,128]{2,0,1...) while((s32[]{:T(128)}, ...), condition=%wide.region_4.5_spmd.clone, body=%wide.region_1.4_spmd.clone.sunk | while | flops 545292160 | bytes 16846516 | solution.py:57
  142.7 2.6 fusion.85
  161.4 2.6 fusion.85
  180.0 2.6 fusion.85
  186.3 2.6 fusion.85
  192.5 2.6 fusion.85
  198.7 2.6 fusion.85
  211.1 2.6 fusion.85
  229.8 2.6 fusion.85
  236.0 2.6 fusion.85
  242.2 2.6 fusion.85
  248.5 2.6 fusion.85
  254.7 2.6 fusion.85
  260.9 2.6 fusion.85
  279.5 2.6 fusion.85
  298.2 2.6 fusion.85
  316.9 2.6 fusion.85
  323.1 2.6 fusion.85
  360.4 2.6 fusion.85
  366.6 2.6 fusion.85
  441.2 2.6 fusion.85
  459.8 2.6 fusion.85
  466.1 2.6 fusion.85
  490.9 2.6 fusion.85
  503.4 2.6 fusion.85
  509.6 2.6 fusion.85
  515.8 2.6 fusion.85
  522.0 2.6 fusion.85
  528.2 2.6 fusion.85
  533.9 4.6 reduce.2
  538.5 5.8 reshape.206
  544.3 4.9 all-to-all-start.1
  549.2 38.1 %fusion.45 = f32[1024,4096]{1,0:T(8,128)} fusion(bf16[3584,4096]{1,0:T(8,128)(2,1)} %param.21, bf16[1024,3584]{1,0:T(8,128)(2,1)} %multiply_convert_fusion.clone.4), kind=kOutput, calls=%fused_computation.31 | convolution fusion | flops 30064771072 | bytes 53477376 | tf_op jit(solution)/shard_map/dot_general | solution.py:35
  587.3 6.8 reshape.207
  596.6 2.6 copy.25
  599.2 16.1 %fusion.61 = f32[1024,4096]{1,0:T(8,128)} fusion(bf16[1024,1024]{0,1:T(8,128)(2,1)} %bitcast.117, bf16[1024,4096]{1,0:T(8,128)(2,1)} %param.18), kind=kOutput, calls=%fused_computation.52 | convolution fusion | flops 8589934592 | bytes 27262976 | tf_op jit(solution)/shard_map/dot_general | solution.py:90
  615.4 562.0 %all-reduce.3.cloned.1.call-done = (f32[1024,4096]{1,0:T(8,128)}, f32[1024,4096]{1,0:T(8,128)}) async-done(((f32[1024,4096]{1,0:T(8,128)}, f32[1024,4096]{1,0:T(8,128)}), (f32[1024,4096]{1,0:T(8,128)}, f32[1024,4096]{1,0:T(8,128)})) %all-reduce.3.cloned.1.call-update) | async-done | bytes 33554448 | tf_op jit(solution)/shard_map/psum | solution.py:91
  1177.4 17.8 %fusion.44 = bf16[1024,4096]{1,0:T(8,128)(2,1)} fusion(f32[1024,4096]{1,0:T(8,128)} %get-tuple-element.73, f32[1024,4096]{1,0:T(8,128)} %get-tuple-element.74, bf16[1024,4096]{1,0:T(8,128)(2,1)} %param.12), kind=kLoop, calls=%fused_computation.29 | loop fusion | flops 16777216 | bytes 50331648 | tf_op jit(solution)/shard_map/convert_element_type | solution.py:92
  (321 shorter events, 287.1 us)
Async XLA Ops:
  7.2 6.4 copy-start
  7.2 6.4 copy-start.3
  7.2 6.4 copy-start.5
  13.6 2.9 copy-start.4
  39.3 82.0 %all-to-all-start = ((bf16[1024,8,3,128]{0,3,2,1:T(8,128)(2,1)}), bf16[1024,8,3,128]{0,3,2,1:T(8,128)(2,1)}, u32[]{:S(2)}, u32[]{:S(2)}) async-start(bf16[1024,8,3,128]{0,3,2,1:T(8,128)(2,1)} %pad_maximum_fusion), calls=%async_computation | async-start | bytes 12582912 | tf_op jit(solution)/shard_map/all_to_all | solution.py:83
  533.3 54.0 %copy-start.2 = (bf16[8192,1,128]{2,0,1:T(8,128)(2,1)}, bf16[8192,1,128]{2,0,1:T(8,128)(2,1)S(1)}, u32[]{:S(2)}) copy-start(bf16[8192,1,128]{2,0,1:T(8,128)(2,1)S(1)} %get-tuple-element.161) | copy-start | bytes 6291460
  544.3 43.0 %all-to-all-start.1 = ((bf16[8,2,65536]{2,1,0:T(2,128)(2,1)}), bf16[8,2,65536]{2,1,0:T(2,128)(2,1)}, u32[]{:S(2)}, u32[]{:S(2)}) async-start(bf16[8,2,65536]{2,1,0:T(2,128)(2,1)} %reshape.206), calls=%async_computation.1 | async-start | bytes 4194304 | tf_op jit(solution)/shard_map/all_to_all | solution.py:89
  549.2 628.2 %all-reduce.3.cloned.1.call-start = ((), (), s32[]{:S(2)}) async-start(), calls=%async_computation.2 | async-start | bytes 67108864 | tf_op jit(solution)/shard_map/psum | solution.py:91
  1177.4 17.8 %copy-start.1 = (bf16[4096,256]{1,0:T(8,128)(2,1)S(1)}, bf16[4096,256]{1,0:T(8,128)(2,1)}, u32[]{:S(2)}) copy-start(bf16[4096,256]{1,0:T(8,128)(2,1)} %param.17) | copy-start | bytes 6291460
Sparse Core Ops, SparseCore 0:
  615.5 561.8 all-reduce.2
where the time goes:
time: 1210 us; the launch traced here: 1200 us
  waiting for transfers between devices  562 us (46%)
  matrix products  410 us (34%)
  other arithmetic  82.8 us (7%)
  local copies, waits for them, and re-layouts  75 us (6%)
  loops' own time  45.7 us (4%)
  between operations  14.7 us (1%)
    psum x1, waiting for transfers between devices, layer_block(): mlp_sum = lax.psum(gated_mlp(normed, w_gate, w_up, w_down), 'tp')  562 us
    dot_general x64, matrix products, attend_tile(): jnp.einsum('qcgd,kcd->cgqk', q_tile, k_keys, preferred_element_type=jnp.f...  164 us
    dot_general x64, matrix products, attend_tile(): jnp.einsum('cgqk,kcd->qcgd', weights.astype(jnp.bfloat16), v_keys, prefer...  96.8 us
    reduce_sum x64, other arithmetic, attend_tile(): weight_total = jnp.sum(weights, axis=-1)  48.8 us
    another operation x1, loops' own time, causal_attention(): attn_tiles = lax.map(attend_tile, jnp.arange(tokens_q // tile_rows))  45.7 us
    dynamic_slice x64, local copies, waits for them, and re-layouts, causal_attention(): attn_tiles = lax.map(attend_tile, jnp.arange(tokens_q // tile_rows))  42.4 us
    dot_general x1, matrix products, gated_mlp(): up_acc = jnp.dot(normed, w_up, preferred_element_type=jnp.float32)  39.3 us
    dot_general x1, matrix products, gated_mlp(): return jnp.dot(hidden, w_down, preferred_element_type=jnp.float32)  38.1 us
  transfers between devices with their start and end apart: 3, of which 1 were waited for; matrix products, arithmetic and copies ran while one was open for 9% of the time, Pallas kernels for 0%

commit v1 on v0

v1 whole, which is shorter than its diff:
```python
import functools
import math

import jax
import jax.numpy as jnp
from jax import lax
from jax.experimental import pallas as pl
from jax.experimental.pallas import tpu as pltpu
from jax.sharding import PartitionSpec as P

HEAD_DIM = 128
EPS = 1e-6
ROPE_BASE = 500000.0
SCORE_SCALE = HEAD_DIM ** -0.5
EXP2_SCALE = SCORE_SCALE * math.log2(math.e)
VMEM_LIMIT = 60 * 1024 * 1024
CHUNKS = 4
ROW_GROUP = 32


def rope_tables(positions):
    inv_freq = ROPE_BASE ** (-(jnp.arange(HEAD_DIM // 2, dtype=jnp.float32) * (2.0 / HEAD_DIM)))
    angles = positions.astype(jnp.float32)[:, None] * inv_freq[None, :]
    cos_tab, sin_tab = jnp.cos(angles), jnp.sin(angles)
    return jnp.concatenate([cos_tab, cos_tab], axis=-1), jnp.concatenate([-sin_tab, sin_tab], axis=-1)


def qkv_kernel(x_ref, g_ref, wq_ref, wk_ref, wv_ref, cos_ref, sin_ref, u_ref, send_ref):
    dests = send_ref.shape[0]
    kv_heads = wk_ref.shape[1] // HEAD_DIM
    repeat = dests // kv_heads
    x = x_ref[...].astype(jnp.float32)
    inv_rms = lax.rsqrt(jnp.mean(x * x, axis=-1, keepdims=True) + EPS)
    u_ref[...] = (x * inv_rms * g_ref[...]).astype(jnp.bfloat16)
    u = u_ref[...]
    cos, sin = cos_ref[...], sin_ref[...]

    def rotate(c):
        return (c * cos + pltpu.roll(c, HEAD_DIM // 2, 1) * sin).astype(jnp.bfloat16)

    q = jnp.dot(u, wq_ref[...], preferred_element_type=jnp.float32)
    for h in range(dests):
        send_ref[h, 0] = rotate(q[:, h * HEAD_DIM:(h + 1) * HEAD_DIM])
    k = jnp.dot(u, wk_ref[...], preferred_element_type=jnp.float32)
    v = jnp.dot(u, wv_ref[...], preferred_element_type=jnp.float32)
    for h in range(kv_heads):
        k_rot = rotate(k[:, h * HEAD_DIM:(h + 1) * HEAD_DIM])
        v_val = v[:, h * HEAD_DIM:(h + 1) * HEAD_DIM].astype(jnp.bfloat16)
        for r in range(repeat):
            send_ref[h * repeat + r, 1] = k_rot
            send_ref[h * repeat + r, 2] = v_val


def qkv_call(x_in, gain, w_q, w_k, w_v, cos, sin, dests):
    rows, width = x_in.shape
    tile = 256
    fixed = functools.partial(pl.BlockSpec, pipeline_mode=pl.Buffered(1))
    cols = w_q.shape[1] + w_k.shape[1] + w_v.shape[1]
    return pl.pallas_call(
        qkv_kernel,
        name="qkv_rope",
        grid=(rows // tile,),
        in_specs=[
            pl.BlockSpec((tile, width), lambda i: (i, 0)),
            fixed((1, width), lambda i: (0, 0)),
            fixed(w_q.shape, lambda i: (0, 0)),
            fixed(w_k.shape, lambda i: (0, 0)),
            fixed(w_v.shape, lambda i: (0, 0)),
            pl.BlockSpec((tile, HEAD_DIM), lambda i: (i, 0)),
            pl.BlockSpec((tile, HEAD_DIM), lambda i: (i, 0)),
        ],
        out_specs=[
            pl.BlockSpec((tile, width), lambda i: (i, 0)),
            pl.BlockSpec((dests, 3, tile, HEAD_DIM), lambda i: (0, 0, i, 0)),
        ],
        out_shape=[
            jax.ShapeDtypeStruct((rows, width), jnp.bfloat16),
            jax.ShapeDtypeStruct((dests, 3, rows, HEAD_DIM), jnp.bfloat16),
        ],
        compiler_params=pltpu.CompilerParams(vmem_limit_bytes=VMEM_LIMIT),
        cost_estimate=pl.CostEstimate(flops=2 * rows * width * cols, bytes_accessed=2 * (2 * rows * width + width * cols), transcendentals=0),
    )(x_in, gain, w_q, w_k, w_v, cos, sin)


def gate_up_kernel(u_ref, w1_ref, w3_ref, h_ref):
    u = u_ref[...]
    gate = jnp.dot(u, w1_ref[...], preferred_element_type=jnp.float32)
    up = jnp.dot(u, w3_ref[...], preferred_element_type=jnp.float32)
    h_ref[...] = (jax.nn.silu(gate) * up).astype(jnp.bfloat16)


def gate_up_call(u, w_gate, w_up):
    rows, width = u.shape
    cols = w_gate.shape[1]
    tile = 256
    return pl.pallas_call(
        gate_up_kernel,
        name="gate_up",
        grid=(cols // tile,),
        in_specs=[
            pl.BlockSpec((rows, width), lambda i: (0, 0), pipeline_mode=pl.Buffered(1)),
            pl.BlockSpec((width, tile), lambda i: (0, i)),
            pl.BlockSpec((width, tile), lambda i: (0, i)),
        ],
        out_specs=pl.BlockSpec((rows, tile), lambda i: (0, i)),
        out_shape=jax.ShapeDtypeStruct((rows, cols), jnp.bfloat16),
        compiler_params=pltpu.CompilerParams(vmem_limit_bytes=VMEM_LIMIT),
        cost_estimate=pl.CostEstimate(flops=4 * rows * width * cols, bytes_accessed=4 * width * cols + 2 * rows * (width + cols), transcendentals=rows * cols),
    )(u, w_gate, w_up)


def flash_kernel(q_ref, k_ref, v_ref, o_ref, s_buf, p_buf, alpha_buf, m_ref, l_ref, acc_ref, *, chunk, stride):
    src = pl.program_id(0)
    strips, strip_rows = q_ref.shape[2], q_ref.shape[3]
    rows = strips * strip_rows
    cols = k_ref.shape[2]
    q = q_ref[0, 0].reshape(rows, HEAD_DIM)

    def source_of(t):
        return jnp.where(t == 0, src, t - 1)

    def scores(t, slot):
        s_buf[slot] = lax.dot_general(q, k_ref[source_of(t), 0], (((1,), (1,)), ((), ())), preferred_element_type=jnp.float32)

    def soften(slot, masked):
        for r in range(0, rows, ROW_GROUP):
            group = pl.ds(r, ROW_GROUP)
            s = [s_buf[slot, group, pl.ds(g, HEAD_DIM)] for g in range(0, cols, HEAD_DIM)]
            if masked:
                row_id = lax.broadcasted_iota(jnp.int32, (ROW_GROUP, HEAD_DIM), 0) + (r // strip_rows * stride + chunk * strip_rows + r % strip_rows)
                col_id = lax.broadcasted_iota(jnp.int32, (ROW_GROUP, HEAD_DIM), 1)
                s = [jnp.where(col_id + g * HEAD_DIM <= row_id, s_g, -jnp.inf) for g, s_g in enumerate(s)]
            top = s[0]
            for s_g in s[1:]:
                top = jnp.maximum(top, s_g)
            top = jnp.broadcast_to(jnp.max(top, axis=1, keepdims=True), (ROW_GROUP, HEAD_DIM))
            if masked:
                alpha_buf[slot, group] = jnp.ones_like(top)
                total = jnp.zeros_like(top)
            else:
                m_old = m_ref[group]
                top = jnp.maximum(m_old, top)
                alpha = jnp.exp2((m_old - top) * EXP2_SCALE)
                alpha_buf[slot, group] = alpha
                total = l_ref[group] * alpha
            m_ref[group] = top
            for g, s_g in enumerate(s):
                p = jnp.exp2((s_g - top) * EXP2_SCALE)
                total = total + p
                p_buf[slot, group, pl.ds(g * HEAD_DIM, HEAD_DIM)] = p.astype(jnp.bfloat16)
            l_ref[group] = total

    def values(t, slot):
        acc_ref[...] = acc_ref[...] * alpha_buf[slot] + jnp.dot(p_buf[slot], v_ref[source_of(t), 0], preferred_element_type=jnp.float32)

    acc_ref[...] = jnp.zeros_like(acc_ref)
    scores(0, 0)
    scores(jnp.minimum(src, 1), 1)
    soften(0, True)

    def step(t, carry):
        for now in range(2):
            @pl.when(t % 2 == now)
            def _():
                scores(jnp.minimum(t + 1, src), 1 - now)
                soften(now, False)
                values(t - 1, 1 - now)
        return carry

    lax.fori_loop(1, src + 1, step, 0)
    for now in range(2):
        @pl.when(src % 2 == now)
        def _():
            values(src, now)
    o_ref[0] = (acc_ref[...] / jnp.sum(l_ref[...], axis=1, keepdims=True)).astype(jnp.bfloat16)


def flash_call(recv, chunk, strips, strip_rows):
    srcs, _, per_src, _ = recv.shape
    rows = strips * strip_rows
    work = srcs * rows * (srcs * per_src // 2)
    by_strip = recv.reshape(srcs, 3, strips, per_src // strips, HEAD_DIM)
    return pl.pallas_call(
        functools.partial(flash_kernel, chunk=chunk, stride=per_src // strips),
        name="flash",
        grid=(srcs,),
        in_specs=[
            pl.BlockSpec((1, 1, strips, strip_rows, HEAD_DIM), lambda s: (s, 0, 0, chunk, 0)),
            pl.BlockSpec((srcs, 1, per_src, HEAD_DIM), lambda s: (0, 1, 0, 0), pipeline_mode=pl.Buffered(1)),
            pl.BlockSpec((srcs, 1, per_src, HEAD_DIM), lambda s: (0, 2, 0, 0), pipeline_mode=pl.Buffered(1)),
        ],
        out_specs=pl.BlockSpec((1, rows, HEAD_DIM), lambda s: (s, 0, 0)),
        out_shape=jax.ShapeDtypeStruct((srcs, rows, HEAD_DIM), jnp.bfloat16),
        scratch_shapes=[
            pltpu.VMEM((2, rows, per_src), jnp.float32),
            pltpu.VMEM((2, rows, per_src), jnp.bfloat16),
            pltpu.VMEM((2, rows, HEAD_DIM), jnp.float32),
            pltpu.VMEM((rows, HEAD_DIM), jnp.float32),
            pltpu.VMEM((rows, HEAD_DIM), jnp.float32),
            pltpu.VMEM((rows, HEAD_DIM), jnp.float32),
        ],
        compiler_params=pltpu.CompilerParams(vmem_limit_bytes=VMEM_LIMIT),
        cost_estimate=pl.CostEstimate(flops=8 * work * HEAD_DIM, bytes_accessed=6 * srcs * per_src * HEAD_DIM, transcendentals=work),
    )(by_strip, recv, recv)


def down_out_kernel(h_ref, a_ref, wd_ref, wo_ref, o_ref):
    a = jnp.concatenate([a_ref[i] for i in range(a_ref.shape[0])], axis=1)
    attn = jnp.dot(a, wo_ref[...], preferred_element_type=jnp.float32)
    hidden = h_ref[...].reshape(a.shape[0], h_ref.shape[2])
    o_ref[...] = attn + jnp.dot(hidden, wd_ref[...], preferred_element_type=jnp.float32)


def down_out_call(hidden, a_heads, w_down, w_o, chunk, strips):
    heads, rows, _ = a_heads.shape
    ff, width = w_down.shape
    tile = 512
    depth = ff + w_o.shape[0]
    return pl.pallas_call(
        down_out_kernel,
        name="down_out",
        grid=(width // tile,),
        in_specs=[
            pl.BlockSpec((strips, rows // strips, ff), lambda i: (0, chunk, 0), pipeline_mode=pl.Buffered(1)),
            pl.BlockSpec((heads, rows, HEAD_DIM), lambda i: (0, 0, 0), pipeline_mode=pl.Buffered(1)),
            pl.BlockSpec((ff, tile), lambda i: (0, i)),
            pl.BlockSpec((w_o.shape[0], tile), lambda i: (0, i)),
        ],
        out_specs=pl.BlockSpec((rows, tile), lambda i: (0, i)),
        out_shape=jax.ShapeDtypeStruct((rows, width), jnp.float32),
        compiler_params=pltpu.CompilerParams(vmem_limit_bytes=VMEM_LIMIT),
        cost_estimate=pl.CostEstimate(flops=2 * rows * depth * width, bytes_accessed=2 * depth * width + 2 * rows * depth + 4 * rows * width, transcendentals=0),
    )(hidden.reshape(strips, hidden.shape[0] // strips, ff), a_heads, w_down, w_o)


def solution(mesh):
    sp_size = mesh.shape["sp"]
    tp_size = mesh.shape["tp"]
    row_spec = P(("rep", "sp"), None)
    cache_spec = P("rep", ("tp", "sp"), None)

    def layer_block(x_in, positions, norm_gain, w_q, w_k, w_v, w_o, w_gate, w_up, w_down):
        tok_local, width = x_in.shape
        cos, sin = rope_tables(positions)
        u, send = qkv_call(x_in, norm_gain[None, :], w_q, w_k, w_v, cos, sin, sp_size)
        recv = lax.all_to_all(send, "sp", 0, 0, tiled=True)
        hidden = gate_up_call(u, w_gate, w_up)
        recv, hidden = lax.optimization_barrier((recv, hidden))
        strip_rows = tok_local // (CHUNKS * tp_size)
        sums = []
        for c in range(CHUNKS):
            attn = flash_call(recv, c, tp_size, strip_rows)
            a_heads = lax.all_to_all(attn, "sp", 0, 0, tiled=True)
            partial = down_out_call(hidden, a_heads, w_down, w_o, c, tp_size)
            sums.append(lax.psum_scatter(partial, "tp", scatter_dimension=0, tiled=True))
        shard = tok_local // tp_size
        x_mine = lax.dynamic_slice_in_dim(x_in, lax.axis_index("tp") * shard, shard, axis=0)
        y_mine = (x_mine.astype(jnp.float32) + jnp.concatenate(sums, axis=0)).astype(jnp.bfloat16)
        y_out = lax.all_gather(y_mine, "tp", axis=0, tiled=True)
        k_all = recv[:, 1].reshape(sp_size * tok_local, 1, HEAD_DIM)
        v_all = recv[:, 2].reshape(sp_size * tok_local, 1, HEAD_DIM)
        return y_out, k_all, v_all

    return jax.shard_map(
        layer_block,
        mesh=mesh,
        in_specs=(row_spec, P(("rep", "sp")), P(None), P(None, "tp"), P(None, "tp"), P(None, "tp"), P("tp", None), P(None, "tp"), P(None, "tp"), P("tp", None)),
        out_specs=(row_spec, cache_spec, cache_spec),
        check_vma=False,
    )
```

time: 1210 us -> 496 us (0.41)
  waiting for transfers between devices: 562 us -> 124 us
  matrix products: 410 us -> 0 us
  Pallas kernels: 0 us -> 273 us
  other arithmetic: 82.8 us -> 8.66 us
  local copies, waits for them, and re-layouts: 75 us -> 12.5 us
  blocking collectives: 0 us -> 57.3 us
  loops' own time: 45.7 us -> 0 us
    psum x1 -> x0, waiting for transfers between devices: 562 us -> none  [layer_block(): mlp_sum = lax.psum(gated_mlp(normed, w_gate, w_up, w_down), 'tp')]
    dot_general x135 -> x0, matrix products: 410 us -> none  [the longest x64 164 us: attend_tile(): jnp.einsum('qcgd,kcd->cgqk', q_tile, k_keys, preferred_element_type=jnp.f...]
    pallas_call x0 -> x10, Pallas kernels: none -> 273 us  [the longest x4 104 us: flash_call(): pl.pallas_call(functools.partial(flash_kernel, chunk=chunk, stride=per_sr...]
    all_gather x0 -> x1, waiting for transfers between devices: none -> 76 us  [layer_block(): y_out = lax.all_gather(y_mine, 'tp', axis=0, tiled=True)]
    all_to_all x0 -> x4, blocking collectives: none -> 57.3 us  [layer_block(): a_heads = lax.all_to_all(attn, 'sp', 0, 0, tiled=True)]
    reduce_sum x65 -> x0, other arithmetic: 54.3 us -> none  [the longest x64 48.8 us: attend_tile(): weight_total = jnp.sum(weights, axis=-1)]
    another operation x1 -> x0, loops' own time: 45.7 us -> none  [causal_attention(): attn_tiles = lax.map(attend_tile, jnp.arange(tokens_q // tile_rows))]
    reduce_scatter x0 -> x4, waiting for transfers between devices: none -> 45 us  [layer_block(): lax.psum_scatter(partial, 'tp', scatter_dimension=0, tiled=True)]
  transfers between devices with their start and end apart: 3 -> 6, of which waited for: 1 -> 3; matrix products, arithmetic and copies ran while one was open for 9% -> 1% of each run, Pallas kernels for 0% -> 41%
where the time goes in v1:
time: 496 us
  Pallas kernels  273 us (55%)
  waiting for transfers between devices  124 us (25%)
  blocking collectives  57.3 us (12%)
  between operations  13.8 us (3%)
  local copies, waits for them, and re-layouts  12.5 us (3%)
  other arithmetic  8.66 us (2%)
  starting transfers between devices  6.98 us (1%)
    pallas_call x4, Pallas kernels, flash_call(): pl.pallas_call(functools.partial(flash_kernel, chunk=chunk, stride=per_sr...  104 us
    pallas_call x4, Pallas kernels, down_out_call(): pl.pallas_call(down_out_kernel, name='down_out', grid=(width // tile,), i...  76.6 us
    all_gather x1, waiting for transfers between devices, layer_block(): y_out = lax.all_gather(y_mine, 'tp', axis=0, tiled=True)  76 us
    pallas_call x1, Pallas kernels, gate_up_call(): pl.pallas_call(gate_up_kernel, name='gate_up', grid=(cols // tile,), in_s...  68.7 us
    all_to_all x4, blocking collectives, layer_block(): a_heads = lax.all_to_all(attn, 'sp', 0, 0, tiled=True)  57.3 us
    reduce_scatter x4, waiting for transfers between devices, layer_block(): lax.psum_scatter(partial, 'tp', scatter_dimension=0, tiled=True)  45 us
    pallas_call x1, Pallas kernels, qkv_call(): pl.pallas_call(qkv_kernel, name='qkv_rope', grid=(rows // tile,), in_spec...  23.7 us
  transfers between devices with their start and end apart: 6, of which 3 were waited for; matrix products, arithmetic and copies ran while one was open for 1% of the time, Pallas kernels for 41%

profile of v1, /device:TPU:97, one launch (start us, length us, event | category | flops | bytes accessed | tf_op | source)
XLA Modules:
  0.0 495.7 jit_solution(9461022144846774018)
XLA Ops:
  7.2 0.7 convert_element_type.10
  7.9 1.9 fusion.1
  9.8 1.3 pad_maximum_fusion
  11.1 23.7 %qkv_rope.1 = (bf16[1024,4096]{1,0:T(8,128)(2,1)}, bf16[8,3,1024,128]{3,2,1,0:T(8,128)(2,1)}) custom-call(bf16[1024,4096]{1,0:T(8,128)(2,1)} %x_ref.1, f32[1,4096]{1,0:T(1,128)} %bitcast.11, bf16[4096,1024]{1,0:T(8,128)(2,1)} %wq_ref.1, bf16[4096,256]{1,0:T(8,128)(2,1)} %wk_ref.1, bf16[4096,256]{1,0:T(8,128)(2,1)} %wv_ref.1, ...), custom_call_target="tpu_custom_call" | custom-call | flops 12884901888 | bytes 29360128 | tf_op jit(solution)/shard_map/qkv_rope/pallas_call | solution.py:59
  34.8 6.7 %all-to-all-start = ((bf16[8,3,1024,128]{3,2,1,0:T(8,128)(2,1)}), bf16[8,3,1024,128]{3,2,1,0:T(8,128)(2,1)}, u32[]{:S(2)}, u32[]{:S(2)}) async-start(bf16[8,3,1024,128]{3,2,1,0:T(8,128)(2,1)} %get-tuple-element.7), calls=%async_computation | async-start | bytes 12582912 | tf_op jit(solution)/shard_map/all_to_all | solution.py:246
  41.5 0.0 reduce-scatter.5.cloned.1.call-start
  41.5 68.7 %gate_up.1 = bf16[1024,3584]{1,0:T(8,128)(2,1)} custom-call(bf16[1024,4096]{1,0:T(8,128)(2,1)} %get-tuple-element.8.u_ref, bf16[4096,3584]{1,0:T(8,128)(2,1)} %w1_ref.1, bf16[4096,3584]{1,0:T(8,128)(2,1)} %w3_ref.1), custom_call_target="tpu_custom_call" | custom-call | flops 60129542144 | bytes 74448896 | tf_op jit(solution)/shard_map/gate_up/pallas_call | solution.py:96
  110.3 2.4 all-to-all-done.k_ref.v_ref
  112.7 25.8 %flash.4 = bf16[8,256,128]{2,1,0:T(8,128)(2,1)} custom-call(bf16[8,3,4,256,128]{4,3,2,1,0:T(8,128)(2,1)} %bitcast.2.q_ref, bf16[8,3,1024,128]{3,2,1,0:T(8,128)(2,1)} %all-to-all-done.k_ref.v_ref, bf16[8,3,1024,128]{3,2,1,0:T(8,128)(2,1)} %all-to-all-done.k_ref.v_ref), custom_call_target="tpu_custom_call" | custom-call | flops 8589934592 | bytes 6291456 | tf_op jit(solution)/shard_map/flash/pallas_call | solution.py:183
  138.5 14.3 %all_to_all.25.a_ref = bf16[8,256,128]{2,1,0:T(8,128)(2,1)} all-to-all(bf16[8,256,128]{2,1,0:T(8,128)(2,1)} %flash.4), channel_id=1, replica_groups=mesh['rep'=1,'tp'=4,'sp'=8] {'sp'}, dimensions={0} | all-to-all | bytes 1048576 | tf_op jit(solution)/shard_map/all_to_all | solution.py:253
  152.8 19.1 %down_out.4 = f32[256,4096]{1,0:T(8,128)} custom-call(bf16[4,256,3584]{2,1,0:T(8,128)(2,1)} %bitcast.5, bf16[8,256,128]{2,1,0:T(8,128)(2,1)} %all_to_all.25.a_ref, bf16[3584,4096]{1,0:T(8,128)(2,1)} %wd_ref.7, bf16[1024,4096]{1,0:T(8,128)(2,1)} %wo_ref.7), custom_call_target="tpu_custom_call" | custom-call | flops 9663676416 | bytes 44302336 | tf_op jit(solution)/shard_map/down_out/pallas_call | solution.py:219
  171.9 0.1 reduce-scatter.5.cloned.1.call-update
  172.0 0.1 reduce-scatter.7.cloned.1.call-start
  172.0 25.9 %flash.5 = bf16[8,256,128]{2,1,0:T(8,128)(2,1)} custom-call(bf16[8,3,4,256,128]{4,3,2,1,0:T(8,128)(2,1)} %bitcast.2.q_ref, bf16[8,3,1024,128]{3,2,1,0:T(8,128)(2,1)} %all-to-all-done.k_ref.v_ref, bf16[8,3,1024,128]{3,2,1,0:T(8,128)(2,1)} %all-to-all-done.k_ref.v_ref), custom_call_target="tpu_custom_call" | custom-call | flops 8589934592 | bytes 6291456 | tf_op jit(solution)/shard_map/flash/pallas_call | solution.py:183
  197.9 14.3 %all_to_all.26.a_ref = bf16[8,256,128]{2,1,0:T(8,128)(2,1)} all-to-all(bf16[8,256,128]{2,1,0:T(8,128)(2,1)} %flash.5), channel_id=1, replica_groups=mesh['rep'=1,'tp'=4,'sp'=8] {'sp'}, dimensions={0} | all-to-all | bytes 1048576 | tf_op jit(solution)/shard_map/all_to_all | solution.py:253
  212.3 19.2 %down_out.5 = f32[256,4096]{1,0:T(8,128)} custom-call(bf16[4,256,3584]{2,1,0:T(8,128)(2,1)} %bitcast.6, bf16[8,256,128]{2,1,0:T(8,128)(2,1)} %all_to_all.26.a_ref, bf16[3584,4096]{1,0:T(8,128)(2,1)} %wd_ref.7, bf16[1024,4096]{1,0:T(8,128)(2,1)} %wo_ref.7), custom_call_target="tpu_custom_call" | custom-call | flops 9663676416 | bytes 44302336 | tf_op jit(solution)/shard_map/down_out/pallas_call | solution.py:219
  231.5 0.1 reduce-scatter.7.cloned.1.call-update
  231.5 0.1 reduce-scatter.11.cloned.1.call-start
  231.6 25.9 %flash.7 = bf16[8,256,128]{2,1,0:T(8,128)(2,1)} custom-call(bf16[8,3,4,256,128]{4,3,2,1,0:T(8,128)(2,1)} %bitcast.2.q_ref, bf16[8,3,1024,128]{3,2,1,0:T(8,128)(2,1)} %all-to-all-done.k_ref.v_ref, bf16[8,3,1024,128]{3,2,1,0:T(8,128)(2,1)} %all-to-all-done.k_ref.v_ref), custom_call_target="tpu_custom_call" | custom-call | flops 8589934592 | bytes 6291456 | tf_op jit(solution)/shard_map/flash/pallas_call | solution.py:183
  257.6 14.3 %all_to_all.27.a_ref = bf16[8,256,128]{2,1,0:T(8,128)(2,1)} all-to-all(bf16[8,256,128]{2,1,0:T(8,128)(2,1)} %flash.7), channel_id=1, replica_groups=mesh['rep'=1,'tp'=4,'sp'=8] {'sp'}, dimensions={0} | all-to-all | bytes 1048576 | tf_op jit(solution)/shard_map/all_to_all | solution.py:253
  271.9 19.1 %down_out.7 = f32[256,4096]{1,0:T(8,128)} custom-call(bf16[4,256,3584]{2,1,0:T(8,128)(2,1)} %bitcast.7, bf16[8,256,128]{2,1,0:T(8,128)(2,1)} %all_to_all.27.a_ref, bf16[3584,4096]{1,0:T(8,128)(2,1)} %wd_ref.7, bf16[1024,4096]{1,0:T(8,128)(2,1)} %wo_ref.7), custom_call_target="tpu_custom_call" | custom-call | flops 9663676416 | bytes 44302336 | tf_op jit(solution)/shard_map/down_out/pallas_call | solution.py:219
  291.0 0.1 reduce-scatter.11.cloned.1.call-update
  291.1 0.1 reduce-scatter.9.cloned.1.call-start
  291.2 25.9 %flash.6 = bf16[8,256,128]{2,1,0:T(8,128)(2,1)} custom-call(bf16[8,3,4,256,128]{4,3,2,1,0:T(8,128)(2,1)} %bitcast.2.q_ref, bf16[8,3,1024,128]{3,2,1,0:T(8,128)(2,1)} %all-to-all-done.k_ref.v_ref, bf16[8,3,1024,128]{3,2,1,0:T(8,128)(2,1)} %all-to-all-done.k_ref.v_ref), custom_call_target="tpu_custom_call" | custom-call | flops 8589934592 | bytes 6291456 | tf_op jit(solution)/shard_map/flash/pallas_call | solution.py:183
  317.1 14.3 %all_to_all.28.a_ref = bf16[8,256,128]{2,1,0:T(8,128)(2,1)} all-to-all(bf16[8,256,128]{2,1,0:T(8,128)(2,1)} %flash.6), channel_id=1, replica_groups=mesh['rep'=1,'tp'=4,'sp'=8] {'sp'}, dimensions={0} | all-to-all | bytes 1048576 | tf_op jit(solution)/shard_map/all_to_all | solution.py:253
  331.4 19.2 %down_out.6 = f32[256,4096]{1,0:T(8,128)} custom-call(bf16[4,256,3584]{2,1,0:T(8,128)(2,1)} %bitcast.8, bf16[8,256,128]{2,1,0:T(8,128)(2,1)} %all_to_all.28.a_ref, bf16[3584,4096]{1,0:T(8,128)(2,1)} %wd_ref.7, bf16[1024,4096]{1,0:T(8,128)(2,1)} %wo_ref.7), custom_call_target="tpu_custom_call" | custom-call | flops 9663676416 | bytes 44302336 | tf_op jit(solution)/shard_map/down_out/pallas_call | solution.py:219
  350.6 0.1 reduce-scatter.9.cloned.1.call-update
  350.7 0.1 all-gather.2.cloned.1.call-start
  350.7 0.0 reduce-scatter.5.cloned.1.call-done
  350.8 0.0 reduce-scatter.7.cloned.1.call-done
  350.8 0.0 reduce-scatter.11.cloned.1.call-done
  350.8 45.0 %reduce-scatter.9.cloned.1.call-done = f32[64,4096]{1,0:T(8,128)} async-done(((f32[256,4096]{1,0:T(8,128)}), f32[64,4096]{1,0:T(8,128)}) %reduce-scatter.9.cloned.1.call-update) | async-done | bytes 1048592 | tf_op jit(solution)/shard_map/reduce_scatter | solution.py:255
  395.8 4.8 fusion
  400.6 0.1 all-gather.2.cloned.1.call-update
  400.6 4.6 fusion.2
  405.3 76.0 %all-gather.2.cloned.1.call-done = bf16[1024,4096]{1,0:T(8,128)(2,1)} async-done(((bf16[256,4096]{1,0:T(8,128)(2,1)}), bf16[1024,4096]{1,0:T(8,128)(2,1)}) %all-gather.2.cloned.1.call-update) | async-done | bytes 8388624 | tf_op jit(solution)/shard_map/all_gather | solution.py:259
  481.3 7.9 %copy.14 = bf16[1024,4096]{1,0:T(8,128)(2,1)} copy(bf16[1024,4096]{1,0:T(8,128)(2,1)} %all-gather.2.cloned.1.call-done) | data formatting | bytes 16777216
  (1 shorter events, 0.0 us)
Async XLA Ops:
  34.8 77.9 %all-to-all-start = ((bf16[8,3,1024,128]{3,2,1,0:T(8,128)(2,1)}), bf16[8,3,1024,128]{3,2,1,0:T(8,128)(2,1)}, u32[]{:S(2)}, u32[]{:S(2)}) async-start(bf16[8,3,1024,128]{3,2,1,0:T(8,128)(2,1)} %get-tuple-element.7), calls=%async_computation | async-start | bytes 12582912 | tf_op jit(solution)/shard_map/all_to_all | solution.py:246
  41.5 309.2 %reduce-scatter.5.cloned.1.call-start = ((), (), s32[]{:S(2)}) async-start(), calls=%async_computation.9 | async-start | bytes 5242880 | tf_op jit(solution)/shard_map/reduce_scatter | solution.py:255
  172.0 178.8 %reduce-scatter.7.cloned.1.call-start = ((), (), s32[]{:S(2)}) async-start(), calls=%async_computation.10 | async-start | bytes 5242880 | tf_op jit(solution)/shard_map/reduce_scatter | solution.py:255
  231.5 119.3 %reduce-scatter.11.cloned.1.call-start = ((), (), s32[]{:S(2)}) async-start(), calls=%async_computation.12 | async-start | bytes 5242880 | tf_op jit(solution)/shard_map/reduce_scatter | solution.py:255
  291.1 104.7 %reduce-scatter.9.cloned.1.call-start = ((), (), s32[]{:S(2)}) async-start(), calls=%async_computation.11 | async-start | bytes 5242880 | tf_op jit(solution)/shard_map/reduce_scatter | solution.py:255
  350.7 130.6 %all-gather.2.cloned.1.call-start = ((), (), s32[]{:S(2)}) async-start(), calls=%async_computation.13 | async-start | bytes 10485760 | tf_op jit(solution)/shard_map/all_gather | solution.py:259
Sparse Core Ops, SparseCore 0:
  172.1 44.9 reduce-scatter.4
  231.7 44.9 reduce-scatter.6
  291.2 44.9 reduce-scatter.10
  350.8 44.9 reduce-scatter.8
  400.7 80.4 all-gather.1

commit v2 on v1

--- a/solution.py
+++ b/solution.py
@@ -15,6 +15,7 @@
 EXP2_SCALE = SCORE_SCALE * math.log2(math.e)
 VMEM_LIMIT = 60 * 1024 * 1024
 CHUNKS = 4
+MESH = pl.DeviceIdType.MESH
 ROW_GROUP = 32
 
 
@@ -109,8 +110,40 @@
     )(u, w_gate, w_up)
 
 
-def flash_kernel(q_ref, k_ref, v_ref, o_ref, s_buf, p_buf, alpha_buf, m_ref, l_ref, acc_ref, *, chunk, stride):
-    src = pl.program_id(0)
+def flash_kernel(q_ref, k_ref, v_ref, out_ref, tiles, s_buf, p_buf, alpha_buf, m_ref, l_ref, acc_ref, send_sem, recv_sem, own_sem, *, chunk, stride):
+    srcs = k_ref.shape[0]
+    here = pl.program_id(0)
+    src = srcs - 1 - here
+    me = lax.axis_index("sp")
+
+    def to_peer(dest):
+        return pltpu.make_async_remote_copy(
+            src_ref=tiles.at[dest], dst_ref=out_ref.at[me], send_sem=send_sem.at[dest], recv_sem=recv_sem.at[me],
+            device_id={"sp": dest}, device_id_type=MESH)
+
+    def to_self():
+        return pltpu.make_async_copy(tiles.at[me], out_ref.at[me], own_sem)
+
+    def send(dest):
+        @pl.when(dest == me)
+        def _():
+            to_self().start()
+
+        @pl.when(dest != me)
+        def _():
+            to_peer(dest).start()
+
+    @pl.when(here == 0)
+    def _():
+        barrier = pltpu.get_barrier_semaphore()
+        for j in range(1, srcs):
+            pl.semaphore_signal(barrier, inc=1, device_id={"sp": lax.rem(me + j, srcs)}, device_id_type=MESH)
+        pl.semaphore_wait(barrier, srcs - 1)
+
+    @pl.when(here > 0)
+    def _():
+        send(src + 1)
+
     strips, strip_rows = q_ref.shape[2], q_ref.shape[3]
     rows = strips * strip_rows
     cols = k_ref.shape[2]
@@ -172,7 +205,25 @@
         @pl.when(src % 2 == now)
         def _():
             values(src, now)
-    o_ref[0] = (acc_ref[...] / jnp.sum(l_ref[...], axis=1, keepdims=True)).astype(jnp.bfloat16)
+    tiles[src] = (acc_ref[...] / jnp.sum(l_ref[...], axis=1, keepdims=True)).astype(jnp.bfloat16)
+
+    @pl.when(here == srcs - 1)
+    def _():
+        for dest in range(1, srcs):
+            @pl.when(dest != me)
+            def _():
+                to_peer(dest).wait_send()
+        send(0)
+
+        @pl.when(me != 0)
+        def _():
+            to_peer(0).wait_send()
+        to_self().wait()
+        for j in range(1, srcs):
+            peer = lax.rem(me + j, srcs)
+            pltpu.make_async_remote_copy(
+                src_ref=tiles.at[0], dst_ref=out_ref.at[peer], send_sem=send_sem.at[0], recv_sem=recv_sem.at[peer],
+                device_id={"sp": peer}, device_id_type=MESH).wait_recv()
 
 
 def flash_call(recv, chunk, strips, strip_rows):
@@ -185,21 +236,25 @@
         name="flash",
         grid=(srcs,),
         in_specs=[
-            pl.BlockSpec((1, 1, strips, strip_rows, HEAD_DIM), lambda s: (s, 0, 0, chunk, 0)),
+            pl.BlockSpec((1, 1, strips, strip_rows, HEAD_DIM), lambda s: (srcs - 1 - s, 0, 0, chunk, 0)),
             pl.BlockSpec((srcs, 1, per_src, HEAD_DIM), lambda s: (0, 1, 0, 0), pipeline_mode=pl.Buffered(1)),
             pl.BlockSpec((srcs, 1, per_src, HEAD_DIM), lambda s: (0, 2, 0, 0), pipeline_mode=pl.Buffered(1)),
         ],
-        out_specs=pl.BlockSpec((1, rows, HEAD_DIM), lambda s: (s, 0, 0)),
+        out_specs=pl.BlockSpec(memory_space=pl.ANY),
         out_shape=jax.ShapeDtypeStruct((srcs, rows, HEAD_DIM), jnp.bfloat16),
         scratch_shapes=[
+            pltpu.VMEM((srcs, rows, HEAD_DIM), jnp.bfloat16),
             pltpu.VMEM((2, rows, per_src), jnp.float32),
             pltpu.VMEM((2, rows, per_src), jnp.bfloat16),
             pltpu.VMEM((2, rows, HEAD_DIM), jnp.float32),
             pltpu.VMEM((rows, HEAD_DIM), jnp.float32),
             pltpu.VMEM((rows, HEAD_DIM), jnp.float32),
             pltpu.VMEM((rows, HEAD_DIM), jnp.float32),
-        ],
-        compiler_params=pltpu.CompilerParams(vmem_limit_bytes=VMEM_LIMIT),
+            pltpu.SemaphoreType.DMA((srcs,)),
+            pltpu.SemaphoreType.DMA((srcs,)),
+            pltpu.SemaphoreType.DMA,
+        ],
+        compiler_params=pltpu.CompilerParams(vmem_limit_bytes=VMEM_LIMIT, collective_id=chunk, has_side_effects=True),
         cost_estimate=pl.CostEstimate(flops=8 * work * HEAD_DIM, bytes_accessed=6 * srcs * per_src * HEAD_DIM, transcendentals=work),
     )(by_strip, recv, recv)
 
@@ -233,6 +288,66 @@
     )(hidden.reshape(strips, hidden.shape[0] // strips, ff), a_heads, w_down, w_o)
 
 
+def gather_kernel(*refs, pieces, n, base):
+    own, out_ref = refs[:pieces], refs[pieces]
+    send_sem, recv_sem, own_sem = refs[pieces + 1:]
+    me = lax.axis_index("tp")
+    right, left = lax.rem(me + 1, n), lax.rem(me + n - 1, n)
+    half = own[0].shape[0] // 2
+    barrier = pltpu.get_barrier_semaphore()
+    for peer in (left, right):
+        pl.semaphore_signal(barrier, inc=1, device_id={"tp": peer}, device_id_type=MESH)
+    pl.semaphore_wait(barrier, 2)
+
+    def hop(h, i, way):
+        peer = right if way == 0 else left
+        owner = lax.rem(me + (n - h if way == 0 else h), n)
+        rows = pl.ds(way * half, half)
+        place = out_ref.at[owner, base + i, rows]
+        return pltpu.make_async_remote_copy(
+            src_ref=own[i].at[rows] if h == 0 else place, dst_ref=place,
+            send_sem=send_sem.at[way, h, i], recv_sem=recv_sem.at[way, h, i],
+            device_id={"tp": peer}, device_id_type=MESH)
+
+    for i in range(pieces):
+        for way in range(2):
+            hop(0, i, way).start()
+    for i in range(pieces):
+        pltpu.make_async_copy(own[i], out_ref.at[me, base + i], own_sem.at[i]).start()
+    for h in range(1, n):
+        for i in range(pieces):
+            for way in range(2):
+                hop(h - 1, i, way).wait_recv()
+                if h < n - 1:
+                    hop(h, i, way).start()
+    for h in range(n - 1):
+        for i in range(pieces):
+            for way in range(2):
+                hop(h, i, way).wait_send()
+    for i in range(pieces):
+        pltpu.make_async_copy(own[i], out_ref.at[me, base + i], own_sem.at[i]).wait()
+
+
+def gather_call(own, n, slots, base, collective_id):
+    rows, width = own[0].shape
+    pieces = len(own)
+    moved = 2 * (n - 1) * pieces * rows * width
+    return pl.pallas_call(
+        functools.partial(gather_kernel, pieces=pieces, n=n, base=base),
+        name="gather_tp",
+        in_specs=[pl.BlockSpec(memory_space=pltpu.VMEM)] * pieces,
+        out_specs=pl.BlockSpec(memory_space=pl.ANY),
+        out_shape=jax.ShapeDtypeStruct((n, slots, rows, width), jnp.bfloat16),
+        scratch_shapes=[
+            pltpu.SemaphoreType.DMA((2, n - 1, pieces)),
+            pltpu.SemaphoreType.DMA((2, n - 1, pieces)),
+            pltpu.SemaphoreType.DMA((pieces,)),
+        ],
+        compiler_params=pltpu.CompilerParams(vmem_limit_bytes=VMEM_LIMIT, collective_id=collective_id, has_side_effects=True),
+        cost_estimate=pl.CostEstimate(flops=moved * 1000, bytes_accessed=moved, transcendentals=0),
+    )(*own)
+
+
 def solution(mesh):
     sp_size = mesh.shape["sp"]
     tp_size = mesh.shape["tp"]
@@ -247,16 +362,22 @@
         hidden = gate_up_call(u, w_gate, w_up)
         recv, hidden = lax.optimization_barrier((recv, hidden))
         strip_rows = tok_local // (CHUNKS * tp_size)
+        shard = tok_local // tp_size
+        x_mine = lax.dynamic_slice_in_dim(x_in, lax.axis_index("tp") * shard, shard, axis=0)
         sums = []
         for c in range(CHUNKS):
-            attn = flash_call(recv, c, tp_size, strip_rows)
-            a_heads = lax.all_to_all(attn, "sp", 0, 0, tiled=True)
+            a_heads = flash_call(recv, c, tp_size, strip_rows)
             partial = down_out_call(hidden, a_heads, w_down, w_o, c, tp_size)
             sums.append(lax.psum_scatter(partial, "tp", scatter_dimension=0, tiled=True))
-        shard = tok_local // tp_size
-        x_mine = lax.dynamic_slice_in_dim(x_in, lax.axis_index("tp") * shard, shard, axis=0)
-        y_mine = (x_mine.astype(jnp.float32) + jnp.concatenate(sums, axis=0)).astype(jnp.bfloat16)
-        y_out = lax.all_gather(y_mine, "tp", axis=0, tiled=True)
+
+        def finish(c, x_rows, total):
+            return (x_rows[c * strip_rows:(c + 1) * strip_rows].astype(jnp.float32) + total).astype(jnp.bfloat16)
+
+        y_early, _ = lax.optimization_barrier(([finish(c, x_mine, sums[c]) for c in range(CHUNKS - 1)], partial))
+        early = gather_call(y_early, tp_size, CHUNKS - 1, 0, CHUNKS)
+        x_late, early = lax.optimization_barrier((x_mine, early))
+        last = gather_call([finish(CHUNKS - 1, x_late, sums[-1])], tp_size, 1, 0, CHUNKS + 1)
+        y_out = jnp.concatenate([early, last], axis=1).reshape(tok_local, width)
         k_all = recv[:, 1].reshape(sp_size * tok_local, 1, HEAD_DIM)
         v_all = recv[:, 2].reshape(sp_size * tok_local, 1, HEAD_DIM)
         return y_out, k_all, v_all

time: 496 us -> 463 us (0.933)
  Pallas kernels: 273 us -> 413 us
  waiting for transfers between devices: 124 us -> 2.67 us
  blocking collectives: 57.3 us -> 0 us
  other arithmetic: 8.66 us -> 17.2 us
  local copies, waits for them, and re-layouts: 12.5 us -> 6.37 us
    pallas_call x0 -> x2, Pallas kernels: none -> 105 us  [gather_call(): pl.pallas_call(functools.partial(gather_kernel, pieces=pieces, n=n, base=...]
    all_gather x1 -> x0, waiting for transfers between devices: 76 us -> none  [layer_block(): y_out = lax.all_gather(y_mine, 'tp', axis=0, tiled=True)]
    all_to_all x4 -> x0, blocking collectives: 57.3 us -> none  [layer_block(): a_heads = lax.all_to_all(attn, 'sp', 0, 0, tiled=True)]
    reduce_scatter x4, waiting for transfers between devices: 45 us -> 0.03 us  [layer_block(): lax.psum_scatter(partial, 'tp', scatter_dimension=0, tiled=True)]
    pallas_call x4, Pallas kernels: 104 us -> 140 us  [flash_call(): pl.pallas_call(functools.partial(flash_kernel, chunk=chunk, stride=per_sr...]
    unnamed x1 -> x0, local copies, waits for them, and re-layouts: 7.89 us -> none
    concatenate x0 -> x1, other arithmetic: none -> 7.55 us  [layer_block(): y_out = jnp.concatenate([early, last], axis=1).reshape(tok_local, width)]
  transfers between devices with their start and end apart: 6 -> 5, of which waited for: 3 -> 1; matrix products, arithmetic and copies ran while one was open for 1% -> 2% of each run, Pallas kernels for 41% -> 69%
where the time goes in v2:
time: 463 us; the launch traced here: 460 us
  Pallas kernels  413 us (89%)
  other arithmetic  17.2 us (4%)
  between operations  13.9 us (3%)
  starting transfers between devices  7.07 us (2%)
  local copies, waits for them, and re-layouts  6.37 us (1%)
    pallas_call x4, Pallas kernels, flash_call(): pl.pallas_call(functools.partial(flash_kernel, chunk=chunk, stride=per_sr...  140 us
    pallas_call x2, Pallas kernels, gather_call(): pl.pallas_call(functools.partial(gather_kernel, pieces=pieces, n=n, base=...  105 us
    pallas_call x4, Pallas kernels, down_out_call(): pl.pallas_call(down_out_kernel, name='down_out', grid=(width // tile,), i...  76.6 us
    pallas_call x1, Pallas kernels, gate_up_call(): pl.pallas_call(gate_up_kernel, name='gate_up', grid=(cols // tile,), in_s...  68.7 us
    pallas_call x1, Pallas kernels, qkv_call(): pl.pallas_call(qkv_kernel, name='qkv_rope', grid=(rows // tile,), in_spec...  23.7 us
  transfers between devices with their start and end apart: 5, of which 1 were waited for; matrix products, arithmetic and copies ran while one was open for 2% of the time, Pallas kernels for 69%

profile of v2, /device:TPU:97, one launch (start us, length us, event | category | flops | bytes accessed | tf_op | source)
XLA Modules:
  0.0 460.4 jit_solution(1994011958071693298)
XLA Ops:
  7.2 0.7 convert_element_type.28
  7.9 1.9 fusion
  9.8 1.3 pad_maximum_fusion.1
  11.1 23.7 %qkv_rope.1 = (bf16[1024,4096]{1,0:T(8,128)(2,1)}, bf16[8,3,1024,128]{3,2,1,0:T(8,128)(2,1)}) custom-call(bf16[1024,4096]{1,0:T(8,128)(2,1)} %x_ref.1, f32[1,4096]{1,0:T(1,128)} %bitcast.13, bf16[4096,1024]{1,0:T(8,128)(2,1)} %wq_ref.1, bf16[4096,256]{1,0:T(8,128)(2,1)} %wk_ref.1, bf16[4096,256]{1,0:T(8,128)(2,1)} %wv_ref.1, ...), custom_call_target="tpu_custom_call" | custom-call | flops 12884901888 | bytes 29360128 | tf_op jit(solution)/shard_map/qkv_rope/pallas_call | solution.py:60
  34.8 6.7 %all-to-all-start = ((bf16[8,3,1024,128]{3,2,1,0:T(8,128)(2,1)}), bf16[8,3,1024,128]{3,2,1,0:T(8,128)(2,1)}, u32[]{:S(2)}, u32[]{:S(2)}) async-start(bf16[8,3,1024,128]{3,2,1,0:T(8,128)(2,1)} %get-tuple-element.12), calls=%async_computation | async-start | bytes 12582912 | tf_op jit(solution)/shard_map/all_to_all | solution.py:361
  41.4 0.0 reduce-scatter.5.cloned.1.call-start
  41.4 68.7 %gate_up.1 = bf16[1024,3584]{1,0:T(8,128)(2,1)} custom-call(bf16[1024,4096]{1,0:T(8,128)(2,1)} %get-tuple-element.13.u_ref, bf16[4096,3584]{1,0:T(8,128)(2,1)} %w1_ref.1, bf16[4096,3584]{1,0:T(8,128)(2,1)} %w3_ref.1), custom_call_target="tpu_custom_call" | custom-call | flops 60129542144 | bytes 74448896 | tf_op jit(solution)/shard_map/gate_up/pallas_call | solution.py:97
  110.1 2.4 all-to-all-done.k_ref.v_ref
  112.6 34.2 %flash.4.a_ref = bf16[8,256,128]{2,1,0:T(8,128)(2,1)} custom-call(bf16[8,3,4,256,128]{4,3,2,1,0:T(8,128)(2,1)} %bitcast.2.q_ref, bf16[8,3,1024,128]{3,2,1,0:T(8,128)(2,1)} %all-to-all-done.k_ref.v_ref, bf16[8,3,1024,128]{3,2,1,0:T(8,128)(2,1)} %all-to-all-done.k_ref.v_ref), custom_call_target="tpu_custom_call" | custom-call | flops 8589934592 | bytes 6291456 | tf_op jit(solution)/shard_map/flash/pallas_call | solution.py:234
  146.7 19.2 %down_out.4 = f32[256,4096]{1,0:T(8,128)} custom-call(bf16[4,256,3584]{2,1,0:T(8,128)(2,1)} %bitcast.6, bf16[8,256,128]{2,1,0:T(8,128)(2,1)} %flash.4.a_ref, bf16[3584,4096]{1,0:T(8,128)(2,1)} %wd_ref.7, bf16[1024,4096]{1,0:T(8,128)(2,1)} %wo_ref.7), custom_call_target="tpu_custom_call" | custom-call | flops 9663676416 | bytes 44302336 | tf_op jit(solution)/shard_map/down_out/pallas_call | solution.py:274
  165.9 0.1 reduce-scatter.5.cloned.1.call-update
  166.0 0.1 reduce-scatter.7.cloned.1.call-start
  166.1 35.1 %flash.5.a_ref = bf16[8,256,128]{2,1,0:T(8,128)(2,1)} custom-call(bf16[8,3,4,256,128]{4,3,2,1,0:T(8,128)(2,1)} %bitcast.2.q_ref, bf16[8,3,1024,128]{3,2,1,0:T(8,128)(2,1)} %all-to-all-done.k_ref.v_ref, bf16[8,3,1024,128]{3,2,1,0:T(8,128)(2,1)} %all-to-all-done.k_ref.v_ref), custom_call_target="tpu_custom_call" | custom-call | flops 8589934592 | bytes 6291456 | tf_op jit(solution)/shard_map/flash/pallas_call | solution.py:234
  201.2 19.2 %down_out.5 = f32[256,4096]{1,0:T(8,128)} custom-call(bf16[4,256,3584]{2,1,0:T(8,128)(2,1)} %bitcast.7, bf16[8,256,128]{2,1,0:T(8,128)(2,1)} %flash.5.a_ref, bf16[3584,4096]{1,0:T(8,128)(2,1)} %wd_ref.7, bf16[1024,4096]{1,0:T(8,128)(2,1)} %wo_ref.7), custom_call_target="tpu_custom_call" | custom-call | flops 9663676416 | bytes 44302336 | tf_op jit(solution)/shard_map/down_out/pallas_call | solution.py:274
  220.3 0.1 reduce-scatter.7.cloned.1.call-update
  220.4 0.1 reduce-scatter.9.cloned.1.call-start
  220.5 35.2 %flash.6.a_ref = bf16[8,256,128]{2,1,0:T(8,128)(2,1)} custom-call(bf16[8,3,4,256,128]{4,3,2,1,0:T(8,128)(2,1)} %bitcast.2.q_ref, bf16[8,3,1024,128]{3,2,1,0:T(8,128)(2,1)} %all-to-all-done.k_ref.v_ref, bf16[8,3,1024,128]{3,2,1,0:T(8,128)(2,1)} %all-to-all-done.k_ref.v_ref), custom_call_target="tpu_custom_call" | custom-call | flops 8589934592 | bytes 6291456 | tf_op jit(solution)/shard_map/flash/pallas_call | solution.py:234
  255.6 19.2 %down_out.6 = f32[256,4096]{1,0:T(8,128)} custom-call(bf16[4,256,3584]{2,1,0:T(8,128)(2,1)} %bitcast.8, bf16[8,256,128]{2,1,0:T(8,128)(2,1)} %flash.6.a_ref, bf16[3584,4096]{1,0:T(8,128)(2,1)} %wd_ref.7, bf16[1024,4096]{1,0:T(8,128)(2,1)} %wo_ref.7), custom_call_target="tpu_custom_call" | custom-call | flops 9663676416 | bytes 44302336 | tf_op jit(solution)/shard_map/down_out/pallas_call | solution.py:274
  274.8 0.1 reduce-scatter.9.cloned.1.call-update
  274.9 0.3 reduce-scatter.11.cloned.1.call-start
  275.2 35.1 %flash.7.a_ref = bf16[8,256,128]{2,1,0:T(8,128)(2,1)} custom-call(bf16[8,3,4,256,128]{4,3,2,1,0:T(8,128)(2,1)} %bitcast.2.q_ref, bf16[8,3,1024,128]{3,2,1,0:T(8,128)(2,1)} %all-to-all-done.k_ref.v_ref, bf16[8,3,1024,128]{3,2,1,0:T(8,128)(2,1)} %all-to-all-done.k_ref.v_ref), custom_call_target="tpu_custom_call" | custom-call | flops 8589934592 | bytes 6291456 | tf_op jit(solution)/shard_map/flash/pallas_call | solution.py:234
  310.3 19.1 %down_out.7 = f32[256,4096]{1,0:T(8,128)} custom-call(bf16[4,256,3584]{2,1,0:T(8,128)(2,1)} %bitcast.9, bf16[8,256,128]{2,1,0:T(8,128)(2,1)} %flash.7.a_ref, bf16[3584,4096]{1,0:T(8,128)(2,1)} %wd_ref.7, bf16[1024,4096]{1,0:T(8,128)(2,1)} %wo_ref.7), custom_call_target="tpu_custom_call" | custom-call | flops 9663676416 | bytes 44302336 | tf_op jit(solution)/shard_map/down_out/pallas_call | solution.py:274
  329.5 0.1 reduce-scatter.11.cloned.1.call-update
  329.5 1.7 constant_dynamic-slice_fusion
  331.3 4.6 %fusion.1 = (bf16[8,1,1024,128]{3,2,1,0:T(8,128)(2,1)}, bf16[8,1,1024,128]{3,2,1,0:T(8,128)(2,1)}) fusion(bf16[8,3,1024,128]{3,2,1,0:T(8,128)(2,1)} %all-to-all-done.k_ref.v_ref), kind=kLoop, calls=%fused_computation.12 | loop fusion | bytes 8388608 | tf_op jit(solution)/shard_map/slice | solution.py:382
  335.9 0.0 reduce-scatter.5.cloned.1.call-done
  335.9 0.0 reduce-scatter.7.cloned.1.call-done
  335.9 0.0 reduce-scatter.9.cloned.1.call-done
  335.9 3.7 add_convert_fusion.1
  339.6 84.8 %gather_tp.2 = bf16[4,3,64,4096]{3,2,1,0:T(8,128)(2,1)} custom-call(bf16[64,4096]{1,0:T(8,128)(2,1)} %get-tuple-element.16.refs_0_, bf16[64,4096]{1,0:T(8,128)(2,1)} %get-tuple-element.17.refs_1_, bf16[64,4096]{1,0:T(8,128)(2,1)} %get-tuple-element.18.refs_2_), custom_call_target="tpu_custom_call" | custom-call | flops 4718592000 | bytes 4718592 | tf_op jit(solution)/shard_map/gather_tp/pallas_call | solution.py:335
  424.4 0.0 reduce-scatter.11.cloned.1.call-done
  424.4 2.1 add_convert_fusion.refs_0_
  426.5 19.8 %gather_tp.3 = bf16[4,1,64,4096]{3,2,1,0:T(8,128)(2,1)} custom-call(bf16[64,4096]{1,0:T(8,128)(2,1)} %add_convert_fusion.refs_0_), custom_call_target="tpu_custom_call" | custom-call | flops 1572864000 | bytes 1572864 | tf_op jit(solution)/shard_map/gather_tp/pallas_call | solution.py:335
  446.3 7.5 %pad_maximum_fusion = bf16[4,4,64,4096]{3,2,1,0:T(8,128)(2,1)} fusion(bf16[4,1,64,4096]{3,2,1,0:T(8,128)(2,1)} %gather_tp.3, bf16[4,3,64,4096]{3,2,1,0:T(8,128)(2,1)} %gather_tp.2), kind=kLoop, calls=%fused_computation | loop fusion | flops 4194304 | bytes 16777216 | tf_op jit(solution)/shard_map/concatenate | solution.py:380
  (1 shorter events, 0.0 us)
Async XLA Ops:
  34.8 77.8 %all-to-all-start = ((bf16[8,3,1024,128]{3,2,1,0:T(8,128)(2,1)}), bf16[8,3,1024,128]{3,2,1,0:T(8,128)(2,1)}, u32[]{:S(2)}, u32[]{:S(2)}) async-start(bf16[8,3,1024,128]{3,2,1,0:T(8,128)(2,1)} %get-tuple-element.12), calls=%async_computation | async-start | bytes 12582912 | tf_op jit(solution)/shard_map/all_to_all | solution.py:361
  41.4 294.5 %reduce-scatter.5.cloned.1.call-start = ((), (), s32[]{:S(2)}) async-start(), calls=%async_computation.5 | async-start | bytes 5242880 | tf_op jit(solution)/shard_map/reduce_scatter | solution.py:371
  166.0 169.9 %reduce-scatter.7.cloned.1.call-start = ((), (), s32[]{:S(2)}) async-start(), calls=%async_computation.6 | async-start | bytes 5242880 | tf_op jit(solution)/shard_map/reduce_scatter | solution.py:371
  220.4 115.5 %reduce-scatter.9.cloned.1.call-start = ((), (), s32[]{:S(2)}) async-start(), calls=%async_computation.7 | async-start | bytes 5242880 | tf_op jit(solution)/shard_map/reduce_scatter | solution.py:371
  274.9 149.5 %reduce-scatter.11.cloned.1.call-start = ((), (), s32[]{:S(2)}) async-start(), calls=%async_computation.8 | async-start | bytes 5242880 | tf_op jit(solution)/shard_map/reduce_scatter | solution.py:371
Sparse Core Ops, SparseCore 0:
  166.1 45.3 reduce-scatter.4
  220.5 45.3 reduce-scatter.6
  275.0 45.3 reduce-scatter.8
  329.6 72.1 reduce-scatter.10

commit v3 on v2

--- a/solution.py
+++ b/solution.py
@@ -15,6 +15,7 @@
 EXP2_SCALE = SCORE_SCALE * math.log2(math.e)
 VMEM_LIMIT = 60 * 1024 * 1024
 CHUNKS = 4
+LAG = 2
 MESH = pl.DeviceIdType.MESH
 ROW_GROUP = 32
 
@@ -113,8 +114,8 @@
 def flash_kernel(q_ref, k_ref, v_ref, out_ref, tiles, s_buf, p_buf, alpha_buf, m_ref, l_ref, acc_ref, send_sem, recv_sem, own_sem, *, chunk, stride):
     srcs = k_ref.shape[0]
     here = pl.program_id(0)
-    src = srcs - 1 - here
     me = lax.axis_index("sp")
+    src = lax.rem(me + 1 + here, srcs)
 
     def to_peer(dest):
         return pltpu.make_async_remote_copy(
@@ -123,15 +124,6 @@
 
     def to_self():
         return pltpu.make_async_copy(tiles.at[me], out_ref.at[me], own_sem)
-
-    def send(dest):
-        @pl.when(dest == me)
-        def _():
-            to_self().start()
-
-        @pl.when(dest != me)
-        def _():
-            to_peer(dest).start()
 
     @pl.when(here == 0)
     def _():
@@ -142,12 +134,12 @@
 
     @pl.when(here > 0)
     def _():
-        send(src + 1)
+        to_peer(lax.rem(me + here, srcs)).start()
 
     strips, strip_rows = q_ref.shape[2], q_ref.shape[3]
     rows = strips * strip_rows
     cols = k_ref.shape[2]
-    q = q_ref[0, 0].reshape(rows, HEAD_DIM)
+    q = q_ref[src, 0].reshape(rows, HEAD_DIM)
 
     def source_of(t):
         return jnp.where(t == 0, src, t - 1)
@@ -209,15 +201,9 @@
 
     @pl.when(here == srcs - 1)
     def _():
-        for dest in range(1, srcs):
-            @pl.when(dest != me)
-            def _():
-                to_peer(dest).wait_send()
-        send(0)
-
-        @pl.when(me != 0)
-        def _():
-            to_peer(0).wait_send()
+        to_self().start()
+        for j in range(1, srcs):
+            to_peer(lax.rem(me + j, srcs)).wait_send()
         to_self().wait()
         for j in range(1, srcs):
             peer = lax.rem(me + j, srcs)
@@ -236,7 +222,7 @@
         name="flash",
         grid=(srcs,),
         in_specs=[
-            pl.BlockSpec((1, 1, strips, strip_rows, HEAD_DIM), lambda s: (srcs - 1 - s, 0, 0, chunk, 0)),
+            pl.BlockSpec((srcs, 1, strips, strip_rows, HEAD_DIM), lambda s: (0, 0, 0, chunk, 0), pipeline_mode=pl.Buffered(1)),
             pl.BlockSpec((srcs, 1, per_src, HEAD_DIM), lambda s: (0, 1, 0, 0), pipeline_mode=pl.Buffered(1)),
             pl.BlockSpec((srcs, 1, per_src, HEAD_DIM), lambda s: (0, 2, 0, 0), pipeline_mode=pl.Buffered(1)),
         ],
@@ -259,56 +245,109 @@
     )(by_strip, recv, recv)
 
 
-def down_out_kernel(h_ref, a_ref, wd_ref, wo_ref, o_ref):
-    a = jnp.concatenate([a_ref[i] for i in range(a_ref.shape[0])], axis=1)
-    attn = jnp.dot(a, wo_ref[...], preferred_element_type=jnp.float32)
-    hidden = h_ref[...].reshape(a.shape[0], h_ref.shape[2])
-    o_ref[...] = attn + jnp.dot(hidden, wd_ref[...], preferred_element_type=jnp.float32)
-
-
-def down_out_call(hidden, a_heads, w_down, w_o, chunk, strips):
-    heads, rows, _ = a_heads.shape
-    ff, width = w_down.shape
-    tile = 512
-    depth = ff + w_o.shape[0]
-    return pl.pallas_call(
-        down_out_kernel,
-        name="down_out",
-        grid=(width // tile,),
-        in_specs=[
-            pl.BlockSpec((strips, rows // strips, ff), lambda i: (0, chunk, 0), pipeline_mode=pl.Buffered(1)),
-            pl.BlockSpec((heads, rows, HEAD_DIM), lambda i: (0, 0, 0), pipeline_mode=pl.Buffered(1)),
-            pl.BlockSpec((ff, tile), lambda i: (0, i)),
-            pl.BlockSpec((w_o.shape[0], tile), lambda i: (0, i)),
-        ],
-        out_specs=pl.BlockSpec((rows, tile), lambda i: (0, i)),
-        out_shape=jax.ShapeDtypeStruct((rows, width), jnp.float32),
-        compiler_params=pltpu.CompilerParams(vmem_limit_bytes=VMEM_LIMIT),
-        cost_estimate=pl.CostEstimate(flops=2 * rows * depth * width, bytes_accessed=2 * depth * width + 2 * rows * depth + 4 * rows * width, transcendentals=0),
-    )(hidden.reshape(strips, hidden.shape[0] // strips, ff), a_heads, w_down, w_o)
-
-
-def gather_kernel(*refs, pieces, n, base):
-    own, out_ref = refs[:pieces], refs[pieces]
-    send_sem, recv_sem, own_sem = refs[pieces + 1:]
+def ring_hops(own, out_ref, send_sem, recv_sem, n, base):
     me = lax.axis_index("tp")
     right, left = lax.rem(me + 1, n), lax.rem(me + n - 1, n)
     half = own[0].shape[0] // 2
-    barrier = pltpu.get_barrier_semaphore()
-    for peer in (left, right):
-        pl.semaphore_signal(barrier, inc=1, device_id={"tp": peer}, device_id_type=MESH)
-    pl.semaphore_wait(barrier, 2)
+
+    def meet():
+        barrier = pltpu.get_barrier_semaphore()
+        for peer in (left, right):
+            pl.semaphore_signal(barrier, inc=1, device_id={"tp": peer}, device_id_type=MESH)
+        pl.semaphore_wait(barrier, 2)
 
     def hop(h, i, way):
-        peer = right if way == 0 else left
         owner = lax.rem(me + (n - h if way == 0 else h), n)
         rows = pl.ds(way * half, half)
         place = out_ref.at[owner, base + i, rows]
         return pltpu.make_async_remote_copy(
             src_ref=own[i].at[rows] if h == 0 else place, dst_ref=place,
             send_sem=send_sem.at[way, h, i], recv_sem=recv_sem.at[way, h, i],
-            device_id={"tp": peer}, device_id_type=MESH)
-
+            device_id={"tp": right if way == 0 else left}, device_id_type=MESH)
+
+    return me, meet, hop
+
+
+def down_out_kernel(*refs, n):
+    h_ref, a_ref, wd_ref, wo_ref = refs[:4]
+    step, last = pl.program_id(0), pl.num_programs(0) - 1
+    if n:
+        own, o_ref, gathered, send_sem, recv_sem, own_sem = refs[4:]
+        me, meet, hop = ring_hops([own], gathered, send_sem, recv_sem, n, 0)
+
+        def keep():
+            return pltpu.make_async_copy(own, gathered.at[me, 0], own_sem)
+
+        @pl.when(step == 0)
+        def _():
+            meet()
+            for way in range(2):
+                hop(0, 0, way).start()
+            keep().start()
+
+        for h in range(1, n - 1):
+            @pl.when(step == jnp.minimum(1 + 2 * h, last))
+            def _():
+                for way in range(2):
+                    hop(h - 1, 0, way).wait_recv()
+                    hop(h, 0, way).start()
+    else:
+        o_ref, = refs[4:]
+    a = jnp.concatenate([a_ref[i] for i in range(a_ref.shape[0])], axis=1)
+    attn = jnp.dot(a, wo_ref[...], preferred_element_type=jnp.float32)
+    hidden = h_ref[...].reshape(a.shape[0], h_ref.shape[2])
+    o_ref[...] = attn + jnp.dot(hidden, wd_ref[...], preferred_element_type=jnp.float32)
+    if n:
+        @pl.when(step == last)
+        def _():
+            for way in range(2):
+                hop(n - 2, 0, way).wait_recv()
+                for h in range(n - 1):
+                    hop(h, 0, way).wait_send()
+            keep().wait()
+
+
+def down_out_call(hidden, a_heads, w_down, w_o, chunk, strips, own=None, collective_id=None):
+    heads, rows, _ = a_heads.shape
+    ff, width = w_down.shape
+    tile = 512
+    depth = ff + w_o.shape[0]
+    in_specs = [
+        pl.BlockSpec((strips, rows // strips, ff), lambda i: (0, chunk, 0), pipeline_mode=pl.Buffered(1)),
+        pl.BlockSpec((heads, rows, HEAD_DIM), lambda i: (0, 0, 0), pipeline_mode=pl.Buffered(1)),
+        pl.BlockSpec((ff, tile), lambda i: (0, i)),
+        pl.BlockSpec((w_o.shape[0], tile), lambda i: (0, i)),
+    ]
+    out_specs = [pl.BlockSpec((rows, tile), lambda i: (0, i))]
+    out_shape = [jax.ShapeDtypeStruct((rows, width), jnp.float32)]
+    operands = [hidden.reshape(strips, hidden.shape[0] // strips, ff), a_heads, w_down, w_o]
+    scratch, n, params = [], 0, {}
+    if own is not None:
+        n = strips
+        in_specs.append(pl.BlockSpec(own.shape, lambda i: (0, 0), pipeline_mode=pl.Buffered(1)))
+        out_specs.append(pl.BlockSpec(memory_space=pl.ANY))
+        out_shape.append(jax.ShapeDtypeStruct((n, 1, *own.shape), own.dtype))
+        operands.append(own)
+        scratch = [pltpu.SemaphoreType.DMA((2, n - 1, 1)), pltpu.SemaphoreType.DMA((2, n - 1, 1)), pltpu.SemaphoreType.DMA]
+        params = {"collective_id": collective_id, "has_side_effects": True}
+    return pl.pallas_call(
+        functools.partial(down_out_kernel, n=n),
+        name="down_out",
+        grid=(width // tile,),
+        in_specs=in_specs,
+        out_specs=out_specs,
+        out_shape=out_shape,
+        scratch_shapes=scratch,
+        compiler_params=pltpu.CompilerParams(vmem_limit_bytes=VMEM_LIMIT, **params),
+        cost_estimate=pl.CostEstimate(flops=2 * rows * depth * width, bytes_accessed=2 * depth * width + 2 * rows * depth + 4 * rows * width, transcendentals=0),
+    )(*operands)
+
+
+def gather_kernel(*refs, pieces, n, base):
+    own, out_ref = refs[:pieces], refs[pieces]
+    send_sem, recv_sem, own_sem = refs[pieces + 1:]
+    me, meet, hop = ring_hops(own, out_ref, send_sem, recv_sem, n, base)
+    meet()
     for i in range(pieces):
         for way in range(2):
             hop(0, i, way).start()
@@ -364,20 +403,29 @@
         strip_rows = tok_local // (CHUNKS * tp_size)
         shard = tok_local // tp_size
         x_mine = lax.dynamic_slice_in_dim(x_in, lax.axis_index("tp") * shard, shard, axis=0)
-        sums = []
-        for c in range(CHUNKS):
-            a_heads = flash_call(recv, c, tp_size, strip_rows)
-            partial = down_out_call(hidden, a_heads, w_down, w_o, c, tp_size)
-            sums.append(lax.psum_scatter(partial, "tp", scatter_dimension=0, tiled=True))
 
         def finish(c, x_rows, total):
             return (x_rows[c * strip_rows:(c + 1) * strip_rows].astype(jnp.float32) + total).astype(jnp.bfloat16)
 
-        y_early, _ = lax.optimization_barrier(([finish(c, x_mine, sums[c]) for c in range(CHUNKS - 1)], partial))
-        early = gather_call(y_early, tp_size, CHUNKS - 1, 0, CHUNKS)
-        x_late, early = lax.optimization_barrier((x_mine, early))
-        last = gather_call([finish(CHUNKS - 1, x_late, sums[-1])], tp_size, 1, 0, CHUNKS + 1)
-        y_out = jnp.concatenate([early, last], axis=1).reshape(tok_local, width)
+        sums, gathered, ids = [], [], iter(range(CHUNKS, 3 * CHUNKS))
+        for c in range(CHUNKS):
+            if c:
+                recv, _ = lax.optimization_barrier((recv, partial))
+            a_heads = flash_call(recv, c, tp_size, strip_rows)
+            if c < LAG:
+                partial, = down_out_call(hidden, a_heads, w_down, w_o, c, tp_size)
+            else:
+                total, a_heads = lax.optimization_barrier((sums[c - LAG], a_heads))
+                own = finish(c - LAG, x_mine, total)
+                partial, moved = down_out_call(hidden, a_heads, w_down, w_o, c, tp_size, own, next(ids))
+                gathered.append(moved)
+            sums.append(lax.psum_scatter(partial, "tp", scatter_dimension=0, tiled=True))
+        waiting = range(CHUNKS - LAG, CHUNKS - 1)
+        x_rest, _ = lax.optimization_barrier((x_mine, partial))
+        early = gather_call([finish(c, x_rest, sums[c]) for c in waiting], tp_size, len(waiting), 0, next(ids))
+        x_late, early = lax.optimization_barrier((x_rest, early))
+        last = gather_call([finish(CHUNKS - 1, x_late, sums[-1])], tp_size, 1, 0, next(ids))
+        y_out = jnp.concatenate([*gathered, early, last], axis=1).reshape(tok_local, width)
         k_all = recv[:, 1].reshape(sp_size * tok_local, 1, HEAD_DIM)
         v_all = recv[:, 2].reshape(sp_size * tok_local, 1, HEAD_DIM)
         return y_out, k_all, v_all

time: 463 us -> 440 us (0.950)
  Pallas kernels: 413 us -> 375 us
  waiting for transfers between devices: 2.67 us -> 16.1 us
    pallas_call x2, Pallas kernels: 105 us -> 60.9 us  [gather_call(): pl.pallas_call(functools.partial(gather_kernel, pieces=pieces, n=n, base=...]
    pallas_call x4, Pallas kernels: 76.6 us -> 103 us  [down_out_call(): pl.pallas_call(functools.partial(down_out_kernel, n=n), name='down_out',...]
    pallas_call x4, Pallas kernels: 140 us -> 119 us  [flash_call(): pl.pallas_call(functools.partial(flash_kernel, chunk=chunk, stride=per_sr...]
    reduce_scatter x4, waiting for transfers between devices: 0.03 us -> 13.5 us  [layer_block(): lax.psum_scatter(partial, 'tp', scatter_dimension=0, tiled=True)]
  transfers between devices with their start and end apart: 5 -> 5, of which waited for: 1 -> 2; matrix products, arithmetic and copies ran while one was open for 2% -> 3% of each run, Pallas kernels for 69% -> 65%
where the time goes in v3:
time: 440 us; the launch traced here: 438 us
  Pallas kernels  375 us (85%)
  other arithmetic  19.3 us (4%)
  waiting for transfers between devices  16.1 us (4%)
  between operations  13.9 us (3%)
  starting transfers between devices  7.06 us (2%)
  local copies, waits for them, and re-layouts  6.38 us (1%)
    pallas_call x4, Pallas kernels, flash_call(): pl.pallas_call(functools.partial(flash_kernel, chunk=chunk, stride=per_sr...  119 us
    pallas_call x4, Pallas kernels, down_out_call(): pl.pallas_call(functools.partial(down_out_kernel, n=n), name='down_out',...  103 us
    pallas_call x1, Pallas kernels, gate_up_call(): pl.pallas_call(gate_up_kernel, name='gate_up', grid=(cols // tile,), in_s...  68.7 us
    pallas_call x2, Pallas kernels, gather_call(): pl.pallas_call(functools.partial(gather_kernel, pieces=pieces, n=n, base=...  60.9 us
    pallas_call x1, Pallas kernels, qkv_call(): pl.pallas_call(qkv_kernel, name='qkv_rope', grid=(rows // tile,), in_spec...  23.7 us
    reduce_scatter x4, waiting for transfers between devices, layer_block(): lax.psum_scatter(partial, 'tp', scatter_dimension=0, tiled=True)  13.5 us
  transfers between devices with their start and end apart: 5, of which 2 were waited for; matrix products, arithmetic and copies ran while one was open for 3% of the time, Pallas kernels for 65%

profile of v3, /device:TPU:97, one launch (start us, length us, event | category | flops | bytes accessed | tf_op | source)
XLA Modules:
  0.0 438.1 jit_solution(3302819927064376416)
XLA Ops:
  7.2 0.7 convert_element_type.27
  7.9 1.9 fusion
  9.8 1.3 pad_maximum_fusion.1
  11.1 23.7 %qkv_rope.1 = (bf16[1024,4096]{1,0:T(8,128)(2,1)}, bf16[8,3,1024,128]{3,2,1,0:T(8,128)(2,1)}) custom-call(bf16[1024,4096]{1,0:T(8,128)(2,1)} %x_ref.1, f32[1,4096]{1,0:T(1,128)} %bitcast.16, bf16[4096,1024]{1,0:T(8,128)(2,1)} %wq_ref.1, bf16[4096,256]{1,0:T(8,128)(2,1)} %wk_ref.1, bf16[4096,256]{1,0:T(8,128)(2,1)} %wv_ref.1, ...), custom_call_target="tpu_custom_call" | custom-call | flops 12884901888 | bytes 29360128 | tf_op jit(solution)/shard_map/qkv_rope/pallas_call | solution.py:61
  34.8 6.6 %all-to-all-start = ((bf16[8,3,1024,128]{3,2,1,0:T(8,128)(2,1)}), bf16[8,3,1024,128]{3,2,1,0:T(8,128)(2,1)}, u32[]{:S(2)}, u32[]{:S(2)}) async-start(bf16[8,3,1024,128]{3,2,1,0:T(8,128)(2,1)} %get-tuple-element.21), calls=%async_computation | async-start | bytes 12582912 | tf_op jit(solution)/shard_map/all_to_all | solution.py:400
  41.4 0.0 reduce-scatter.5.cloned.1.call-start
  41.4 68.7 %gate_up.1 = bf16[1024,3584]{1,0:T(8,128)(2,1)} custom-call(bf16[1024,4096]{1,0:T(8,128)(2,1)} %get-tuple-element.22.u_ref, bf16[4096,3584]{1,0:T(8,128)(2,1)} %w1_ref.1, bf16[4096,3584]{1,0:T(8,128)(2,1)} %w3_ref.1), custom_call_target="tpu_custom_call" | custom-call | flops 60129542144 | bytes 74448896 | tf_op jit(solution)/shard_map/gate_up/pallas_call | solution.py:98
  110.2 2.4 all-to-all-done.k_ref.v_ref
  112.6 28.7 %flash.4.refs_1_ = bf16[8,256,128]{2,1,0:T(8,128)(2,1)} custom-call(bf16[8,3,4,256,128]{4,3,2,1,0:T(8,128)(2,1)} %bitcast.2.q_ref, bf16[8,3,1024,128]{3,2,1,0:T(8,128)(2,1)} %all-to-all-done.k_ref.v_ref, bf16[8,3,1024,128]{3,2,1,0:T(8,128)(2,1)} %all-to-all-done.k_ref.v_ref), custom_call_target="tpu_custom_call" | custom-call | flops 8589934592 | bytes 6291456 | tf_op jit(solution)/shard_map/flash/pallas_call | solution.py:220
  141.2 19.2 %down_out.4 = f32[256,4096]{1,0:T(8,128)} custom-call(bf16[4,256,3584]{2,1,0:T(8,128)(2,1)} %bitcast.9, bf16[8,256,128]{2,1,0:T(8,128)(2,1)} %flash.4.refs_1_, bf16[3584,4096]{1,0:T(8,128)(2,1)} %refs_2_.7, bf16[1024,4096]{1,0:T(8,128)(2,1)} %refs_3_.7), custom_call_target="tpu_custom_call" | custom-call | flops 9663676416 | bytes 44302336 | tf_op jit(solution)/shard_map/down_out/pallas_call | solution.py:333
  160.4 0.1 reduce-scatter.5.cloned.1.call-update
  160.5 0.1 reduce-scatter.7.cloned.1.call-start
  160.5 30.4 %flash.5.refs_1_ = bf16[8,256,128]{2,1,0:T(8,128)(2,1)} custom-call(bf16[8,3,4,256,128]{4,3,2,1,0:T(8,128)(2,1)} %bitcast.3.q_ref, bf16[8,3,1024,128]{3,2,1,0:T(8,128)(2,1)} %all-to-all-done.k_ref.v_ref, bf16[8,3,1024,128]{3,2,1,0:T(8,128)(2,1)} %all-to-all-done.k_ref.v_ref), custom_call_target="tpu_custom_call" | custom-call | flops 8589934592 | bytes 6291456 | tf_op jit(solution)/shard_map/flash/pallas_call | solution.py:220
  191.0 19.1 %down_out.5 = f32[256,4096]{1,0:T(8,128)} custom-call(bf16[4,256,3584]{2,1,0:T(8,128)(2,1)} %bitcast.10, bf16[8,256,128]{2,1,0:T(8,128)(2,1)} %flash.5.refs_1_, bf16[3584,4096]{1,0:T(8,128)(2,1)} %refs_2_.7, bf16[1024,4096]{1,0:T(8,128)(2,1)} %refs_3_.7), custom_call_target="tpu_custom_call" | custom-call | flops 9663676416 | bytes 44302336 | tf_op jit(solution)/shard_map/down_out/pallas_call | solution.py:333
  210.1 0.1 reduce-scatter.7.cloned.1.call-update
  210.2 0.3 reduce-scatter.9.cloned.1.call-start
  210.5 30.5 %flash.6.refs_1_ = bf16[8,256,128]{2,1,0:T(8,128)(2,1)} custom-call(bf16[8,3,4,256,128]{4,3,2,1,0:T(8,128)(2,1)} %bitcast.4.q_ref, bf16[8,3,1024,128]{3,2,1,0:T(8,128)(2,1)} %all-to-all-done.k_ref.v_ref, bf16[8,3,1024,128]{3,2,1,0:T(8,128)(2,1)} %all-to-all-done.k_ref.v_ref), custom_call_target="tpu_custom_call" | custom-call | flops 8589934592 | bytes 6291456 | tf_op jit(solution)/shard_map/flash/pallas_call | solution.py:220
  241.0 0.0 reduce-scatter.5.cloned.1.call-done
  241.0 2.2 add_convert_fusion.3.refs_4_
  243.3 32.8 %down_out.6 = (f32[256,4096]{1,0:T(8,128)}, bf16[4,1,64,4096]{3,2,1,0:T(8,128)(2,1)}) custom-call(bf16[4,256,3584]{2,1,0:T(8,128)(2,1)} %bitcast.11, bf16[8,256,128]{2,1,0:T(8,128)(2,1)} %flash.6.refs_1_, bf16[3584,4096]{1,0:T(8,128)(2,1)} %refs_2_.7, bf16[1024,4096]{1,0:T(8,128)(2,1)} %refs_3_.7, bf16[64,4096]{1,0:T(8,128)(2,1)} %add_convert_fusion.3.refs_4_), custom_call_target="tpu_custom_call" | custom-call | flops 9663676416 | bytes 44302336 | tf_op jit(solution)/shard_map/down_out/pallas_call | solution.py:333
  276.1 0.1 reduce-scatter.9.cloned.1.call-update
  276.1 0.1 reduce-scatter.11.cloned.1.call-start
  276.2 29.4 %flash.7.refs_1_ = bf16[8,256,128]{2,1,0:T(8,128)(2,1)} custom-call(bf16[8,3,4,256,128]{4,3,2,1,0:T(8,128)(2,1)} %bitcast.5.q_ref, bf16[8,3,1024,128]{3,2,1,0:T(8,128)(2,1)} %all-to-all-done.k_ref.v_ref, bf16[8,3,1024,128]{3,2,1,0:T(8,128)(2,1)} %all-to-all-done.k_ref.v_ref), custom_call_target="tpu_custom_call" | custom-call | flops 8589934592 | bytes 6291456 | tf_op jit(solution)/shard_map/flash/pallas_call | solution.py:220
  305.6 0.0 reduce-scatter.7.cloned.1.call-done
  305.7 2.2 add_convert_fusion.2.refs_4_
  307.9 32.0 %down_out.7 = (f32[256,4096]{1,0:T(8,128)}, bf16[4,1,64,4096]{3,2,1,0:T(8,128)(2,1)}) custom-call(bf16[4,256,3584]{2,1,0:T(8,128)(2,1)} %bitcast.12, bf16[8,256,128]{2,1,0:T(8,128)(2,1)} %flash.7.refs_1_, bf16[3584,4096]{1,0:T(8,128)(2,1)} %refs_2_.7, bf16[1024,4096]{1,0:T(8,128)(2,1)} %refs_3_.7, bf16[64,4096]{1,0:T(8,128)(2,1)} %add_convert_fusion.2.refs_4_), custom_call_target="tpu_custom_call" | custom-call | flops 9663676416 | bytes 44302336 | tf_op jit(solution)/shard_map/down_out/pallas_call | solution.py:333
  339.9 0.1 reduce-scatter.11.cloned.1.call-update
  340.0 1.7 constant_dynamic-slice_fusion
  341.7 4.6 %fusion.1 = (bf16[8,1,1024,128]{3,2,1,0:T(8,128)(2,1)}, bf16[8,1,1024,128]{3,2,1,0:T(8,128)(2,1)}) fusion(bf16[8,3,1024,128]{3,2,1,0:T(8,128)(2,1)} %all-to-all-done.k_ref.v_ref), kind=kLoop, calls=%fused_computation.12 | loop fusion | bytes 8388608 | tf_op jit(solution)/shard_map/slice | solution.py:430
  346.3 0.0 reduce-scatter.9.cloned.1.call-done
  346.3 2.1 add_convert_fusion.1.refs_0_
  348.5 40.7 %gather_tp.2 = bf16[4,1,64,4096]{3,2,1,0:T(8,128)(2,1)} custom-call(bf16[64,4096]{1,0:T(8,128)(2,1)} %add_convert_fusion.1.refs_0_), custom_call_target="tpu_custom_call" | custom-call | flops 1572864000 | bytes 1572864 | tf_op jit(solution)/shard_map/gather_tp/pallas_call | solution.py:374
  389.2 13.4 %reduce-scatter.11.cloned.1.call-done = f32[64,4096]{1,0:T(8,128)} async-done(((f32[256,4096]{1,0:T(8,128)}), f32[64,4096]{1,0:T(8,128)}) %reduce-scatter.11.cloned.1.call-update) | async-done | bytes 1048592 | tf_op jit(solution)/shard_map/reduce_scatter | solution.py:422
  402.6 2.1 add_convert_fusion.refs_0_
  404.7 0.0 copy-start
  404.7 20.2 %gather_tp.3 = bf16[4,1,64,4096]{3,2,1,0:T(8,128)(2,1)} custom-call(bf16[64,4096]{1,0:T(8,128)(2,1)} %add_convert_fusion.refs_0_), custom_call_target="tpu_custom_call" | custom-call | flops 1572864000 | bytes 1572864 | tf_op jit(solution)/shard_map/gather_tp/pallas_call | solution.py:374
  424.9 0.0 copy-done
  424.9 6.6 %pad_maximum_fusion = bf16[4,4,64,4096]{3,2,1,0:T(8,128)(2,1)} fusion(bf16[4,1,64,4096]{3,2,1,0:T(8,128)(2,1)} %gather_tp.3, bf16[4,1,64,4096]{3,2,1,0:T(8,128)(2,1)} %gather_tp.2, bf16[4,1,64,4096]{3,2,1,0:T(8,128)(2,1)} %get-tuple-element.34, bf16[4,1,64,4096]{3,2,1,0:T(8,128)(2,1)S(1)} %copy-done), kind=kLoop, calls=%fused_computation | loop fusion | flops 12582912 | bytes 16777216 | tf_op jit(solution)/shard_map/concatenate | solution.py:428
  (1 shorter events, 0.0 us)
Async XLA Ops:
  34.8 77.8 %all-to-all-start = ((bf16[8,3,1024,128]{3,2,1,0:T(8,128)(2,1)}), bf16[8,3,1024,128]{3,2,1,0:T(8,128)(2,1)}, u32[]{:S(2)}, u32[]{:S(2)}) async-start(bf16[8,3,1024,128]{3,2,1,0:T(8,128)(2,1)} %get-tuple-element.21), calls=%async_computation | async-start | bytes 12582912 | tf_op jit(solution)/shard_map/all_to_all | solution.py:400
  41.4 199.6 %reduce-scatter.5.cloned.1.call-start = ((), (), s32[]{:S(2)}) async-start(), calls=%async_computation.5 | async-start | bytes 5242880 | tf_op jit(solution)/shard_map/reduce_scatter | solution.py:422
  160.5 145.2 %reduce-scatter.7.cloned.1.call-start = ((), (), s32[]{:S(2)}) async-start(), calls=%async_computation.6 | async-start | bytes 5242880 | tf_op jit(solution)/shard_map/reduce_scatter | solution.py:422
  210.2 136.2 %reduce-scatter.9.cloned.1.call-start = ((), (), s32[]{:S(2)}) async-start(), calls=%async_computation.7 | async-start | bytes 5242880 | tf_op jit(solution)/shard_map/reduce_scatter | solution.py:422
  276.1 126.5 %reduce-scatter.11.cloned.1.call-start = ((), (), s32[]{:S(2)}) async-start(), calls=%async_computation.8 | async-start | bytes 5242880 | tf_op jit(solution)/shard_map/reduce_scatter | solution.py:422
  404.7 20.2 %copy-start = (bf16[4,1,64,4096]{3,2,1,0:T(8,128)(2,1)S(1)}, bf16[4,1,64,4096]{3,2,1,0:T(8,128)(2,1)}, u32[]{:S(2)}) copy-start(bf16[4,1,64,4096]{3,2,1,0:T(8,128)(2,1)} %get-tuple-element.29) | copy-start | bytes 6291460
Sparse Core Ops, SparseCore 0:
  160.6 46.3 reduce-scatter.4
  210.3 50.0 reduce-scatter.6
  276.2 48.3 reduce-scatter.8
  340.1 62.5 reduce-scatter.10

commit v4 on v3

--- a/solution.py
+++ b/solution.py
@@ -423,11 +423,12 @@
         waiting = range(CHUNKS - LAG, CHUNKS - 1)
         x_rest, _ = lax.optimization_barrier((x_mine, partial))
         early = gather_call([finish(c, x_rest, sums[c]) for c in waiting], tp_size, len(waiting), 0, next(ids))
-        x_late, early = lax.optimization_barrier((x_rest, early))
+        x_rest, early, recv = lax.optimization_barrier((x_rest, early, recv))
+        k_all = recv[:, 1].reshape(sp_size * tok_local, 1, HEAD_DIM)
+        v_all = recv[:, 2].reshape(sp_size * tok_local, 1, HEAD_DIM)
+        x_late, k_all, v_all = lax.optimization_barrier((x_rest, k_all, v_all))
         last = gather_call([finish(CHUNKS - 1, x_late, sums[-1])], tp_size, 1, 0, next(ids))
         y_out = jnp.concatenate([*gathered, early, last], axis=1).reshape(tok_local, width)
-        k_all = recv[:, 1].reshape(sp_size * tok_local, 1, HEAD_DIM)
-        v_all = recv[:, 2].reshape(sp_size * tok_local, 1, HEAD_DIM)
         return y_out, k_all, v_all
 
     return jax.shard_map(

time: 440 us -> 439 us (level)
  transfers between devices with their start and end apart: 5 -> 5, of which waited for: 2 -> 2; matrix products, arithmetic and copies ran while one was open for 3% -> 3% of each run, Pallas kernels for 65% -> 64%
where the time goes in v4:
time: 439 us; the launch traced here: 438 us
  Pallas kernels  374 us (85%)
  other arithmetic  19.3 us (4%)
  waiting for transfers between devices  17.1 us (4%)
  between operations  13.9 us (3%)
  starting transfers between devices  7.06 us (2%)
  local copies, waits for them, and re-layouts  6.38 us (1%)
    pallas_call x4, Pallas kernels, flash_call(): pl.pallas_call(functools.partial(flash_kernel, chunk=chunk, stride=per_sr...  119 us
    pallas_call x4, Pallas kernels, down_out_call(): pl.pallas_call(functools.partial(down_out_kernel, n=n), name='down_out',...  103 us
    pallas_call x1, Pallas kernels, gate_up_call(): pl.pallas_call(gate_up_kernel, name='gate_up', grid=(cols // tile,), in_s...  68.7 us
    pallas_call x2, Pallas kernels, gather_call(): pl.pallas_call(functools.partial(gather_kernel, pieces=pieces, n=n, base=...  59.5 us
    pallas_call x1, Pallas kernels, qkv_call(): pl.pallas_call(qkv_kernel, name='qkv_rope', grid=(rows // tile,), in_spec...  23.7 us
    reduce_scatter x4, waiting for transfers between devices, layer_block(): lax.psum_scatter(partial, 'tp', scatter_dimension=0, tiled=True)  14.5 us
  transfers between devices with their start and end apart: 5, of which 2 were waited for; matrix products, arithmetic and copies ran while one was open for 3% of the time, Pallas kernels for 64%

profile of v4, /device:TPU:97, one launch (start us, length us, event | category | flops | bytes accessed | tf_op | source)
XLA Modules:
  0.0 437.8 jit_solution(12234389854389583994)
XLA Ops:
  7.2 0.7 convert_element_type.27
  7.9 1.9 fusion
  9.8 1.3 pad_maximum_fusion.1
  11.1 23.7 %qkv_rope.1 = (bf16[1024,4096]{1,0:T(8,128)(2,1)}, bf16[8,3,1024,128]{3,2,1,0:T(8,128)(2,1)}) custom-call(bf16[1024,4096]{1,0:T(8,128)(2,1)} %x_ref.1, f32[1,4096]{1,0:T(1,128)} %bitcast.16, bf16[4096,1024]{1,0:T(8,128)(2,1)} %wq_ref.1, bf16[4096,256]{1,0:T(8,128)(2,1)} %wk_ref.1, bf16[4096,256]{1,0:T(8,128)(2,1)} %wv_ref.1, ...), custom_call_target="tpu_custom_call" | custom-call | flops 12884901888 | bytes 29360128 | tf_op jit(solution)/shard_map/qkv_rope/pallas_call | solution.py:61
  34.8 6.6 %all-to-all-start = ((bf16[8,3,1024,128]{3,2,1,0:T(8,128)(2,1)}), bf16[8,3,1024,128]{3,2,1,0:T(8,128)(2,1)}, u32[]{:S(2)}, u32[]{:S(2)}) async-start(bf16[8,3,1024,128]{3,2,1,0:T(8,128)(2,1)} %get-tuple-element.25), calls=%async_computation | async-start | bytes 12582912 | tf_op jit(solution)/shard_map/all_to_all | solution.py:400
  41.4 0.0 reduce-scatter.5.cloned.1.call-start
  41.4 68.7 %gate_up.1 = bf16[1024,3584]{1,0:T(8,128)(2,1)} custom-call(bf16[1024,4096]{1,0:T(8,128)(2,1)} %get-tuple-element.26.u_ref, bf16[4096,3584]{1,0:T(8,128)(2,1)} %w1_ref.1, bf16[4096,3584]{1,0:T(8,128)(2,1)} %w3_ref.1), custom_call_target="tpu_custom_call" | custom-call | flops 60129542144 | bytes 74448896 | tf_op jit(solution)/shard_map/gate_up/pallas_call | solution.py:98
  110.2 2.4 all-to-all-done.k_ref.v_ref
  112.6 28.7 %flash.4.refs_1_ = bf16[8,256,128]{2,1,0:T(8,128)(2,1)} custom-call(bf16[8,3,4,256,128]{4,3,2,1,0:T(8,128)(2,1)} %bitcast.2.q_ref, bf16[8,3,1024,128]{3,2,1,0:T(8,128)(2,1)} %all-to-all-done.k_ref.v_ref, bf16[8,3,1024,128]{3,2,1,0:T(8,128)(2,1)} %all-to-all-done.k_ref.v_ref), custom_call_target="tpu_custom_call" | custom-call | flops 8589934592 | bytes 6291456 | tf_op jit(solution)/shard_map/flash/pallas_call | solution.py:220
  141.2 19.2 %down_out.4 = f32[256,4096]{1,0:T(8,128)} custom-call(bf16[4,256,3584]{2,1,0:T(8,128)(2,1)} %bitcast.9, bf16[8,256,128]{2,1,0:T(8,128)(2,1)} %flash.4.refs_1_, bf16[3584,4096]{1,0:T(8,128)(2,1)} %refs_2_.7, bf16[1024,4096]{1,0:T(8,128)(2,1)} %refs_3_.7), custom_call_target="tpu_custom_call" | custom-call | flops 9663676416 | bytes 44302336 | tf_op jit(solution)/shard_map/down_out/pallas_call | solution.py:333
  160.4 0.1 reduce-scatter.5.cloned.1.call-update
  160.5 0.1 reduce-scatter.7.cloned.1.call-start
  160.5 30.4 %flash.5.refs_1_ = bf16[8,256,128]{2,1,0:T(8,128)(2,1)} custom-call(bf16[8,3,4,256,128]{4,3,2,1,0:T(8,128)(2,1)} %bitcast.3.q_ref, bf16[8,3,1024,128]{3,2,1,0:T(8,128)(2,1)} %all-to-all-done.k_ref.v_ref, bf16[8,3,1024,128]{3,2,1,0:T(8,128)(2,1)} %all-to-all-done.k_ref.v_ref), custom_call_target="tpu_custom_call" | custom-call | flops 8589934592 | bytes 6291456 | tf_op jit(solution)/shard_map/flash/pallas_call | solution.py:220
  191.0 19.1 %down_out.5 = f32[256,4096]{1,0:T(8,128)} custom-call(bf16[4,256,3584]{2,1,0:T(8,128)(2,1)} %bitcast.10, bf16[8,256,128]{2,1,0:T(8,128)(2,1)} %flash.5.refs_1_, bf16[3584,4096]{1,0:T(8,128)(2,1)} %refs_2_.7, bf16[1024,4096]{1,0:T(8,128)(2,1)} %refs_3_.7), custom_call_target="tpu_custom_call" | custom-call | flops 9663676416 | bytes 44302336 | tf_op jit(solution)/shard_map/down_out/pallas_call | solution.py:333
  210.1 0.1 reduce-scatter.7.cloned.1.call-update
  210.2 0.3 reduce-scatter.9.cloned.1.call-start
  210.5 30.5 %flash.6.refs_1_ = bf16[8,256,128]{2,1,0:T(8,128)(2,1)} custom-call(bf16[8,3,4,256,128]{4,3,2,1,0:T(8,128)(2,1)} %bitcast.4.q_ref, bf16[8,3,1024,128]{3,2,1,0:T(8,128)(2,1)} %all-to-all-done.k_ref.v_ref, bf16[8,3,1024,128]{3,2,1,0:T(8,128)(2,1)} %all-to-all-done.k_ref.v_ref), custom_call_target="tpu_custom_call" | custom-call | flops 8589934592 | bytes 6291456 | tf_op jit(solution)/shard_map/flash/pallas_call | solution.py:220
  241.0 0.0 reduce-scatter.5.cloned.1.call-done
  241.0 2.2 add_convert_fusion.3.refs_4_
  243.3 32.8 %down_out.6 = (f32[256,4096]{1,0:T(8,128)}, bf16[4,1,64,4096]{3,2,1,0:T(8,128)(2,1)}) custom-call(bf16[4,256,3584]{2,1,0:T(8,128)(2,1)} %bitcast.11, bf16[8,256,128]{2,1,0:T(8,128)(2,1)} %flash.6.refs_1_, bf16[3584,4096]{1,0:T(8,128)(2,1)} %refs_2_.7, bf16[1024,4096]{1,0:T(8,128)(2,1)} %refs_3_.7, bf16[64,4096]{1,0:T(8,128)(2,1)} %add_convert_fusion.3.refs_4_), custom_call_target="tpu_custom_call" | custom-call | flops 9663676416 | bytes 44302336 | tf_op jit(solution)/shard_map/down_out/pallas_call | solution.py:333
  276.1 0.1 reduce-scatter.9.cloned.1.call-update
  276.1 0.1 reduce-scatter.11.cloned.1.call-start
  276.2 29.5 %flash.7.refs_1_ = bf16[8,256,128]{2,1,0:T(8,128)(2,1)} custom-call(bf16[8,3,4,256,128]{4,3,2,1,0:T(8,128)(2,1)} %bitcast.5.q_ref, bf16[8,3,1024,128]{3,2,1,0:T(8,128)(2,1)} %all-to-all-done.k_ref.v_ref, bf16[8,3,1024,128]{3,2,1,0:T(8,128)(2,1)} %all-to-all-done.k_ref.v_ref), custom_call_target="tpu_custom_call" | custom-call | flops 8589934592 | bytes 6291456 | tf_op jit(solution)/shard_map/flash/pallas_call | solution.py:220
  305.6 0.0 reduce-scatter.7.cloned.1.call-done
  305.7 2.2 add_convert_fusion.2.refs_4_
  307.9 32.0 %down_out.7 = (f32[256,4096]{1,0:T(8,128)}, bf16[4,1,64,4096]{3,2,1,0:T(8,128)(2,1)}) custom-call(bf16[4,256,3584]{2,1,0:T(8,128)(2,1)} %bitcast.12, bf16[8,256,128]{2,1,0:T(8,128)(2,1)} %flash.7.refs_1_, bf16[3584,4096]{1,0:T(8,128)(2,1)} %refs_2_.7, bf16[1024,4096]{1,0:T(8,128)(2,1)} %refs_3_.7, bf16[64,4096]{1,0:T(8,128)(2,1)} %add_convert_fusion.2.refs_4_), custom_call_target="tpu_custom_call" | custom-call | flops 9663676416 | bytes 44302336 | tf_op jit(solution)/shard_map/down_out/pallas_call | solution.py:333
  339.9 0.1 reduce-scatter.11.cloned.1.call-update
  340.0 1.7 constant_dynamic-slice_fusion
  341.7 0.0 reduce-scatter.9.cloned.1.call-done
  341.7 2.1 add_convert_fusion.1.refs_0_
  343.8 37.7 %gather_tp.2 = bf16[4,1,64,4096]{3,2,1,0:T(8,128)(2,1)} custom-call(bf16[64,4096]{1,0:T(8,128)(2,1)} %add_convert_fusion.1.refs_0_), custom_call_target="tpu_custom_call" | custom-call | flops 1572864000 | bytes 1572864 | tf_op jit(solution)/shard_map/gather_tp/pallas_call | solution.py:374
  381.5 4.6 %fusion.1 = (bf16[8,1,1024,128]{3,2,1,0:T(8,128)(2,1)}, bf16[8,1,1024,128]{3,2,1,0:T(8,128)(2,1)}) fusion(bf16[8,3,1024,128]{3,2,1,0:T(8,128)(2,1)} %all-to-all-done.k_ref.v_ref), kind=kLoop, calls=%fused_computation.12 | loop fusion | bytes 8388608 | tf_op jit(solution)/shard_map/slice | solution.py:428
  386.2 14.5 %reduce-scatter.11.cloned.1.call-done = f32[64,4096]{1,0:T(8,128)} async-done(((f32[256,4096]{1,0:T(8,128)}), f32[64,4096]{1,0:T(8,128)}) %reduce-scatter.11.cloned.1.call-update) | async-done | bytes 1048592 | tf_op jit(solution)/shard_map/reduce_scatter | solution.py:422
  400.6 2.1 add_convert_fusion.refs_0_
  402.7 0.0 copy-start
  402.7 21.8 %gather_tp.3 = bf16[4,1,64,4096]{3,2,1,0:T(8,128)(2,1)} custom-call(bf16[64,4096]{1,0:T(8,128)(2,1)} %add_convert_fusion.refs_0_), custom_call_target="tpu_custom_call" | custom-call | flops 1572864000 | bytes 1572864 | tf_op jit(solution)/shard_map/gather_tp/pallas_call | solution.py:374
  424.6 0.0 copy-done
  424.6 6.6 %pad_maximum_fusion = bf16[4,4,64,4096]{3,2,1,0:T(8,128)(2,1)} fusion(bf16[4,1,64,4096]{3,2,1,0:T(8,128)(2,1)} %gather_tp.3, bf16[4,1,64,4096]{3,2,1,0:T(8,128)(2,1)} %gather_tp.2, bf16[4,1,64,4096]{3,2,1,0:T(8,128)(2,1)} %get-tuple-element.38, bf16[4,1,64,4096]{3,2,1,0:T(8,128)(2,1)S(1)} %copy-done), kind=kLoop, calls=%fused_computation | loop fusion | flops 12582912 | bytes 16777216 | tf_op jit(solution)/shard_map/concatenate | solution.py:431
  (1 shorter events, 0.0 us)
Async XLA Ops:
  34.8 77.8 %all-to-all-start = ((bf16[8,3,1024,128]{3,2,1,0:T(8,128)(2,1)}), bf16[8,3,1024,128]{3,2,1,0:T(8,128)(2,1)}, u32[]{:S(2)}, u32[]{:S(2)}) async-start(bf16[8,3,1024,128]{3,2,1,0:T(8,128)(2,1)} %get-tuple-element.25), calls=%async_computation | async-start | bytes 12582912 | tf_op jit(solution)/shard_map/all_to_all | solution.py:400
  41.4 199.6 %reduce-scatter.5.cloned.1.call-start = ((), (), s32[]{:S(2)}) async-start(), calls=%async_computation.5 | async-start | bytes 5242880 | tf_op jit(solution)/shard_map/reduce_scatter | solution.py:422
  160.5 145.2 %reduce-scatter.7.cloned.1.call-start = ((), (), s32[]{:S(2)}) async-start(), calls=%async_computation.6 | async-start | bytes 5242880 | tf_op jit(solution)/shard_map/reduce_scatter | solution.py:422
  210.2 131.5 %reduce-scatter.9.cloned.1.call-start = ((), (), s32[]{:S(2)}) async-start(), calls=%async_computation.7 | async-start | bytes 5242880 | tf_op jit(solution)/shard_map/reduce_scatter | solution.py:422
  276.1 124.5 %reduce-scatter.11.cloned.1.call-start = ((), (), s32[]{:S(2)}) async-start(), calls=%async_computation.8 | async-start | bytes 5242880 | tf_op jit(solution)/shard_map/reduce_scatter | solution.py:422
  402.7 21.9 %copy-start = (bf16[4,1,64,4096]{3,2,1,0:T(8,128)(2,1)S(1)}, bf16[4,1,64,4096]{3,2,1,0:T(8,128)(2,1)}, u32[]{:S(2)}) copy-start(bf16[4,1,64,4096]{3,2,1,0:T(8,128)(2,1)} %get-tuple-element.33) | copy-start | bytes 6291460
Sparse Core Ops, SparseCore 0:
  160.6 46.3 reduce-scatter.4
  210.3 50.0 reduce-scatter.6
  276.2 48.3 reduce-scatter.8
  340.1 60.4 reduce-scatter.10
